TPU v7x, 32 devices: a whole 2x2x4 slice. The times are simulated.
32 devices in a mesh: dp: 16 (over z, y, x), tensor: 2 (over core).
Axes of the slice: x: 2, y: 2, z: 4, core: 2. Of those that a mesh axis runs over, the one named last changes fastest.
Arguments:
- inputs: bfloat16 [16384, 512], P('dp'), may hold values from -6 to 6
- w_qkv: bfloat16 [3, 512, 512], P(None, None, 'tensor'), may hold values from -0.25 to 0.25
- b_qv: float32 [2, 512], P(None, 'tensor'), may hold values from -1.2 to 1.2
- w_out: bfloat16 [512, 512], P('tensor'), may hold values from -3 to 3
- b_out: float32 [512], replicated, may hold values from -3 to 3
- norm1_gain: float32 [512], replicated, may hold values from 0.1 to 1.9
- norm1_shift: float32 [512], replicated, may hold values from -3 to 3
- w_in: bfloat16 [512, 1024], P(None, 'tensor'), may hold values from -0.25 to 0.25
- b_in: float32 [1024], P('tensor'), may hold values from -3 to 3
- w_down: bfloat16 [1024, 512], P('tensor'), may hold values from -0.25 to 0.25
- b_down: float32 [512], replicated, may hold values from -3 to 3
- norm2_gain: float32 [512], replicated, may hold values from 0.1 to 1.9
- norm2_shift: float32 [512], replicated, may hold values from -3 to 3
- segment_ids: int32 [16, 1024], P('dp'), may hold values from 0 to 9, as said below
- d_out: bfloat16 [16384, 512], P(('dp', 'tensor')), may hold values from -6 to 6
Outputs:
- output: bfloat16 [16384, 512], P(('dp', 'tensor'))
- d_inputs: bfloat16 [16384, 512], P(('dp', 'tensor'))
- grad_w_qkv: float32 [3, 512, 512], P(None, None, 'tensor')
- grad_b_qv: float32 [2, 512], P(None, 'tensor')
- grad_w_out: float32 [512, 512], P('tensor')
- grad_b_out: float32 [512], replicated
- grad_norm1_gain: float32 [512], replicated
- grad_norm1_shift: float32 [512], replicated
- grad_w_in: float32 [512, 1024], P(None, 'tensor')
- grad_b_in: float32 [1024], P('tensor')
- grad_w_down: float32 [1024, 512], P('tensor')
- grad_b_down: float32 [512], replicated
- grad_norm2_gain: float32 [512], replicated
- grad_norm2_shift: float32 [512], replicated
Inputs may be any that keep to these rules, and one draw needn't show every extreme that they name: `segment_ids`: along a row the ids never fall until the trailing padding; datasets carry ids 1 to 9, padding carries 0 and stands only at a row's end; row 0 has no padding.
All inputs are finite; a program needn't handle non-finite values.
Results may differ from a plain program's by a relative error of at most 0.02.
Values may be sent and summed in bfloat16 or wider, within the bound.
A program may use at most 64 MiB of HBM per device.

v0:
```python
from functools import partial

import jax
import jax.numpy as jnp
from jax import lax
from jax.sharding import PartitionSpec as P

HD = 128
QBLK = 512


NORM_EPSILON = 1e-05
MASKED_SCORE = -1e30


def layer_norm(values, norm_gain, norm_shift):
    average = jnp.mean(values, -1, keepdims=True)
    centred = values - average
    spread = jnp.mean(centred * centred, -1, keepdims=True)
    return centred * lax.rsqrt(spread + NORM_EPSILON) * norm_gain + norm_shift


def masked_norm(row_mask, pre_norm, norm_gain, norm_shift):
    return layer_norm(pre_norm, norm_gain, norm_shift) * row_mask


def exact_gelu(values):
    return jax.nn.gelu(values, approximate=False)


def take_rows(array, row_from, row_count):
    return lax.dynamic_slice_in_dim(array, row_from, row_count, 0)


def block_scores(query_blk, seg_blk, key_rows, key_segments, score_scale):
    scores = (
        jnp.einsum("qhd,khd->hqk", query_blk, key_rows, preferred_element_type=jnp.float32)
        * score_scale
    )
    matching = seg_blk[:, None] == key_segments[None, :]
    return jnp.where(matching[None], scores, MASKED_SCORE)


def attend_forward(queries, key_rows, values, query_segments, key_segments, score_scale):
    length, heads_local, head_size = queries.shape
    block_count = length // QBLK
    query_blocks = queries.reshape(block_count, QBLK, heads_local, head_size)
    seg_blocks = query_segments.reshape(block_count, QBLK)

    def one_block(pieces):
        query_blk, seg_blk = pieces
        scores = block_scores(query_blk, seg_blk, key_rows, key_segments, score_scale)
        row_max = jnp.max(scores, -1, keepdims=True)
        weights = jnp.exp(scores - row_max)
        row_total = jnp.sum(weights, -1, keepdims=True)
        probs_low = (weights / row_total).astype(jnp.bfloat16)
        mixture = jnp.einsum("hqk,khd->qhd", probs_low, values, preferred_element_type=jnp.float32)
        return (mixture.astype(jnp.bfloat16), (row_max + jnp.log(row_total))[..., 0])

    mixture, log_total = lax.map(one_block, (query_blocks, seg_blocks))
    return (mixture.reshape(length, heads_local * head_size), log_total)


def attend_backward(
    queries, key_rows, values, query_segments, key_segments, log_total, d_mixture, score_scale
):
    length, heads_local, head_size = queries.shape
    block_count = length // QBLK
    query_blocks = queries.reshape(block_count, QBLK, heads_local, head_size)
    seg_blocks = query_segments.reshape(block_count, QBLK)
    grad_blocks = d_mixture.reshape(block_count, QBLK, heads_local, head_size)

    def one_block(sums_carry, pieces):
        key_sum, value_sum = sums_carry
        query_blk, seg_blk, total_blk, grad_blk = pieces
        scores = block_scores(query_blk, seg_blk, key_rows, key_segments, score_scale)
        attn_probs = jnp.exp(scores - total_blk[..., None])
        d_probs = jnp.einsum("qhd,khd->hqk", grad_blk, values, preferred_element_type=jnp.float32)
        row_delta = jnp.sum(attn_probs * d_probs, -1, keepdims=True)
        d_scores = (attn_probs * (d_probs - row_delta)).astype(jnp.bfloat16)
        d_query = (
            jnp.einsum("hqk,khd->qhd", d_scores, key_rows, preferred_element_type=jnp.float32)
            * score_scale
        )
        key_sum = (
            key_sum
            + jnp.einsum("hqk,qhd->khd", d_scores, query_blk, preferred_element_type=jnp.float32)
            * score_scale
        )
        value_sum = value_sum + jnp.einsum(
            "hqk,qhd->khd",
            attn_probs.astype(jnp.bfloat16),
            grad_blk,
            preferred_element_type=jnp.float32,
        )
        return ((key_sum, value_sum), d_query.astype(jnp.bfloat16))

    zero_rows = jnp.zeros(key_rows.shape, jnp.float32)
    (key_sum, value_sum), d_queries = lax.scan(
        one_block, (zero_rows, zero_rows), (query_blocks, seg_blocks, log_total, grad_blocks)
    )
    return (d_queries.reshape(length, heads_local * head_size), key_sum, value_sum)


def feed_forward(hidden_low, w_in, b_in):
    up_proj = jnp.dot(hidden_low, w_in, preferred_element_type=jnp.float32) + b_in
    activated, gelu_back = jax.vjp(exact_gelu, up_proj)
    return (activated.astype(jnp.bfloat16), gelu_back)


def on_device(
    inputs,
    w_qkv,
    b_qv,
    w_out,
    b_out,
    norm1_gain,
    norm1_shift,
    w_in,
    b_in,
    w_down,
    b_down,
    norm2_gain,
    norm2_shift,
    segment_ids,
    d_out,
):
    length = inputs.shape[0]
    half_rows = length // lax.axis_size("tensor")
    row_first = lax.axis_index("tensor") * half_rows
    score_scale = HD ** (-0.5)
    segments = segment_ids[0]
    row_mask = (segments != 0).astype(jnp.float32)[:, None]
    local_width = w_qkv.shape[2]
    heads_local = local_width // HD
    projected = jnp.einsum("td,cde->cte", inputs, w_qkv, preferred_element_type=jnp.float32)
    queries = (projected[0] + b_qv[0]).astype(jnp.bfloat16).reshape(length, heads_local, HD)
    key_rows = projected[1].astype(jnp.bfloat16).reshape(length, heads_local, HD)
    values = (projected[2] + b_qv[1]).astype(jnp.bfloat16).reshape(length, heads_local, HD)
    mixture, log_total = attend_forward(queries, key_rows, values, segments, segments, score_scale)
    attn_partial = jnp.dot(mixture, w_out, preferred_element_type=jnp.float32)
    attn_out = lax.psum(attn_partial.astype(jnp.bfloat16), "tensor").astype(jnp.float32) + b_out
    hidden, norm1_back = jax.vjp(
        layer_norm, inputs.astype(jnp.float32) + attn_out, norm1_gain, norm1_shift
    )
    hidden_low = hidden.astype(jnp.bfloat16)
    act_low, gelu_back = feed_forward(hidden_low, w_in, b_in)
    down_proj = (
        lax.psum(
            jnp.dot(act_low, w_down, preferred_element_type=jnp.float32).astype(jnp.bfloat16),
            "tensor",
        ).astype(jnp.float32)
        + b_down
    )
    result, norm2_back = jax.vjp(
        partial(masked_norm, row_mask), hidden + down_proj, norm2_gain, norm2_shift
    )
    output = take_rows(result, row_first, half_rows).astype(jnp.bfloat16)
    cotangent = lax.all_gather(d_out, "tensor", axis=0, tiled=True).astype(jnp.float32)
    d_resid, grad_norm2_gain, grad_norm2_shift = norm2_back(cotangent)
    d_down = d_resid.astype(jnp.bfloat16)
    grad_b_down = jnp.sum(d_down, 0, dtype=jnp.float32)
    grad_w_down = jnp.einsum("tf,td->fd", act_low, d_down, preferred_element_type=jnp.float32)
    d_act = jnp.einsum("td,fd->tf", d_down, w_down, preferred_element_type=jnp.float32)
    d_up = gelu_back(d_act)[0].astype(jnp.bfloat16)
    grad_b_in = jnp.sum(d_up, 0, dtype=jnp.float32)
    grad_w_in = jnp.einsum("td,tf->df", hidden_low, d_up, preferred_element_type=jnp.float32)
    ffn_partial = jnp.einsum("tf,df->td", d_up, w_in, preferred_element_type=jnp.float32)
    d_hidden = d_resid + lax.psum(ffn_partial.astype(jnp.bfloat16), "tensor").astype(jnp.float32)
    d_pre, grad_norm1_gain, grad_norm1_shift = norm1_back(d_hidden)
    d_attn = d_pre.astype(jnp.bfloat16)
    grad_b_out = jnp.sum(d_attn, 0, dtype=jnp.float32)
    resid_rows = take_rows(d_pre, row_first, half_rows)
    grad_w_out = jnp.einsum("te,td->ed", mixture, d_attn, preferred_element_type=jnp.float32)
    d_mixture = jnp.einsum("td,ed->te", d_attn, w_out, preferred_element_type=jnp.float32).astype(
        jnp.bfloat16
    )
    d_mixture = d_mixture.reshape(length, heads_local, HD)
    d_queries, key_sum, value_sum = attend_backward(
        queries, key_rows, values, segments, segments, log_total, d_mixture, score_scale
    )
    d_keys = key_sum.astype(jnp.bfloat16).reshape(length, local_width)
    d_values = value_sum.astype(jnp.bfloat16).reshape(length, local_width)
    d_proj = jnp.stack([d_queries, d_keys, d_values])
    grad_w_qkv = jnp.einsum("td,cte->cde", inputs, d_proj, preferred_element_type=jnp.float32)
    grad_b_qv = jnp.stack(
        [jnp.sum(d_queries, 0, dtype=jnp.float32), jnp.sum(d_values, 0, dtype=jnp.float32)]
    )
    d_inputs = (
        resid_rows
        + lax.psum_scatter(
            jnp.einsum("cte,cde->td", d_proj, w_qkv, preferred_element_type=jnp.float32).astype(
                jnp.bfloat16
            ),
            "tensor",
            scatter_dimension=0,
            tiled=True,
        ).astype(jnp.float32)
    ).astype(jnp.bfloat16)
    (
        grad_w_qkv,
        grad_b_qv,
        grad_w_out,
        grad_b_out,
        grad_norm1_gain,
        grad_norm1_shift,
        grad_w_in,
        grad_b_in,
        grad_w_down,
        grad_b_down,
        grad_norm2_gain,
        grad_norm2_shift,
    ) = lax.psum(
        (
            grad_w_qkv,
            grad_b_qv,
            grad_w_out,
            grad_b_out,
            grad_norm1_gain,
            grad_norm1_shift,
            grad_w_in,
            grad_b_in,
            grad_w_down,
            grad_b_down,
            grad_norm2_gain,
            grad_norm2_shift,
        ),
        "dp",
    )
    return (
        output,
        d_inputs,
        grad_w_qkv,
        grad_b_qv,
        grad_w_out,
        grad_b_out,
        grad_norm1_gain,
        grad_norm1_shift,
        grad_w_in,
        grad_b_in,
        grad_w_down,
        grad_b_down,
        grad_norm2_gain,
        grad_norm2_shift,
    )


def solution(mesh):
    placed = (
        P("dp", None),
        P(None, None, "tensor"),
        P(None, "tensor"),
        P("tensor", None),
        P(),
        P(),
        P(),
        P(None, "tensor"),
        P("tensor"),
        P("tensor", None),
        P(),
        P(),
        P(),
        P("dp", None),
        P(("dp", "tensor"), None),
    )
    return jax.shard_map(
        on_device,
        mesh=mesh,
        in_specs=placed,
        out_specs=(
            P(("dp", "tensor"), None),
            P(("dp", "tensor"), None),
            P(None, None, "tensor"),
            P(None, "tensor"),
            P("tensor", None),
            P(),
            P(),
            P(),
            P(None, "tensor"),
            P("tensor"),
            P("tensor", None),
            P(),
            P(),
            P(),
        ),
        check_vma=False,
    )
```

profile of v0, /device:TPU:0, one launch (start us, length us, event | category | flops | bytes accessed | tf_op | source)
XLA Modules:
  0.0 373.9 jit_solution(6552756230015744487)
XLA Ops:
  7.3 1.1 copy-done
  8.3 2.2 convolution_bitcast_fusion
  10.7 1.1 fusion.77
  13.6 3.1 squeeze.24
  16.7 2.3 copy.45
  19.0 1.1 copy-done.12
  20.2 10.9 %while.27 = (s32[]{:T(128)}, bf16[2,512,2,128]{3,2,1,0:T(2,128)(2,1)}, f32[2,2,512]{2,1,0:T(2,128)S(1)}, s32[2,512]{1,0:T(2,128)S(1)}, s32[1,1024]{1,0:T(1,128)S...) while((s32[]{:T(128)}, ...), condition=%wide.region_3.4_spmd, body=%wide.region_0.3_spmd.sunk | while | flops 550108160 | bytes 21014700 | solution.py:60
  20.6 1.1 fusion.120
  21.7 1.2 fusion.121
  22.9 1.7 fusion.122
  26.1 1.1 fusion.120
  27.1 1.2 fusion.121
  28.3 1.7 fusion.122
  31.1 2.6 convolution_convert_fusion
  33.8 22.2 %all-reduce.7.cloned.1.call-done = bf16[1024,512]{1,0:T(8,128)(2,1)} async-done(((bf16[1024,512]{1,0:T(8,128)(2,1)}), bf16[1024,512]{1,0:T(8,128)(2,1)}) %all-reduce.7.cloned.1.call-update) | async-done | bytes 1048592 | tf_op jit(solution)/shard_map/psum | solution.py:142
  56.1 1.8 fusion.48
  58.6 7.0 %multiply_convert_fusion.1 = (bf16[1024,512]{1,0:T(8,128)(2,1)S(1)}, f32[1024,512]{1,0:T(8,128)}, f32[1024,512]{1,0:T(8,128)}) fusion(f32[512]{0:T(512)S(1)} %copy-done.45, bf16[512,512]{1,0:T(8,128)(2,1)S(1)} %copy-done.43, f32[512]{0:T(512)S(1)} %copy-done.38, f32[512]{0:T(512)S(1)} %copy-done.35, f32[1024]{0:T(1024)S(1)} %fusion.60, ...), kind=kOutput, calls=%fused_computation.70 | convolution fusion | flops 576192512 | bytes 7880704 | tf_op jit(solution)/shard_map/dot_general | solution.py:106
  65.6 1.0 copy-done.46
  66.5 1.7 convolution_convert_fusion.2
  69.2 19.8 %all-reduce.9.cloned.1.call-done = bf16[1024,512]{1,0:T(8,128)(2,1)} async-done(((bf16[1024,512]{1,0:T(8,128)(2,1)}), bf16[1024,512]{1,0:T(8,128)(2,1)}) %all-reduce.9.cloned.1.call-update) | async-done | bytes 1048592 | tf_op jit(solution)/shard_map/psum | solution.py:149
  89.0 3.8 %fusion.75 = (f32[1024]{0:T(1024)S(1)}, f32[1024,512]{1,0:T(8,128)}) fusion(f32[512]{0:T(512)S(1)} %copy-done.37, bf16[1024,512]{1,0:T(8,128)(2,1)} %all-reduce.9.cloned.1.call-done, f32[512]{0:T(512)S(1)} %copy-done.38, f32[512]{0:T(512)S(1)} %copy-done.35, f32[1024]{0:T(1024)S(1)} %fusion.60, f32[1024]{0:T(1024)S(1)} %broadcast_multiply_fusion.1, ...), kind=kLoop, calls=%fused_computation.138 | loop fusion | flops 6290432 | bytes 5263360 | tf_op jit(solution)/shard_map/jvp()/reduce_sum | solution.py:17
  92.8 8.0 %all-gather.2.cloned.1.call-done = bf16[1024,512]{1,0:T(8,128)(2,1)} async-done(((bf16[512,512]{1,0:T(8,128)(2,1)}), bf16[1024,512]{1,0:T(8,128)(2,1)}) %all-gather.2.cloned.1.call-update) | async-done | bytes 1048592 | tf_op jit(solution)/shard_map/all_gather | solution.py:159
  100.8 3.0 multiply_reduce_fusion.4
  103.8 2.3 fusion.74
  106.4 1.1 copy-done.42
  107.5 1.5 copy-done.49
  109.0 1.4 convert_reduce_fusion.1
  110.5 1.0 copy-done.47
  111.4 1.7 convolution_convert_fusion.1
  113.2 20.7 %all-reduce.11.cloned.1.call-done = bf16[1024,512]{1,0:T(8,128)(2,1)} async-done(((bf16[1024,512]{1,0:T(8,128)(2,1)}), bf16[1024,512]{1,0:T(8,128)(2,1)}) %all-reduce.11.cloned.1.call-update) | async-done | bytes 1048592 | tf_op jit(solution)/shard_map/psum | solution.py:169
  133.9 3.5 fusion.73
  137.4 1.4 multiply_reduce_fusion.2
  138.8 1.2 convert_reduce_fusion.2
  140.0 1.3 copy-done.7
  141.3 1.3 convolution_convert_fusion.3
  142.6 2.0 reshape_reshape.2
  144.6 20.9 %while.28 = (s32[]{:T(128)}, f32[1024,2,128]{0,2,1:T(8,128)}, f32[1024,2,128]{0,2,1:T(8,128)}, bf16[2,512,2,128]{3,1,2,0:T(8,128)(2,1)}, bf16[2,512,2,128]{3,1,2...) while((s32[]{:T(128)}, f32[1024,2,128]{0,2,1:T(8,128)}, ...), condition=%wide.region_17.18_spmd.clone, body=%wide.region_15.17_spmd.clone.sunk | while | flops 1360002048 | bytes 62167372 | solution.py:99
  144.6 1.1 constant_dynamic-slice_fusion.8
  147.3 1.5 fusion.133
  148.8 1.8 multiply_reduce_fusion.8
  150.7 1.3 multiply_convert_fusion.3
  152.1 0.8 fusion.134
  154.1 1.0 copy-done.3
  155.1 1.1 constant_dynamic-slice_fusion.8
  157.8 1.5 fusion.133
  159.3 1.8 multiply_reduce_fusion.8
  161.2 1.3 multiply_convert_fusion.3
  162.5 0.8 fusion.134
  164.5 1.0 copy-done.3
  165.5 1.4 convert_element_type.141
  168.0 1.6 convert_reduce_fusion.3
  169.6 1.0 copy.61
  170.6 3.0 bitcast_convert_fusion
  173.9 3.4 fusion.79
  177.3 2.1 fusion.66
  179.4 1.3 fusion.55
  180.8 2.2 convolution_bitcast_fusion.1
  183.7 2.3 fusion.52
  186.1 79.6 %all-reduce = (f32[2,256]{1,0:T(2,128)}, f32[512]{0:T(512)}, f32[512]{0:T(512)}, f32[512]{0:T(512)}, f32[512]{0:T(512)}, /*index=5*/f32[512]{0:T(512)}, f32[512]{0:T(512)}, f32[512]{0:T(512)}) all-reduce(f32[2,256]{1,0:T(2,128)S(1)} %pad_maximum_fusion.3, ...), channel_id=1, replica_groups=mesh['dp'=16,'tensor'=2] {'dp'}, use_global_device_ids=true, to_apply=%region_22.23 | all-reduce | flops 4096 | bytes 32768 | tf_op jit(solution)/shard_map/psum | solution.py:213
  265.7 2.0 add_convert_fusion.2
  267.7 93.5 %all-reduce.13.cloned.1.call-done = (f32[3,512,256]{1,2,0:T(8,128)}, f32[256,512]{1,0:T(8,128)}, f32[512,512]{1,0:T(8,128)}, f32[512,512]{1,0:T(8,128)}) async-done(((f32[3,512,256]{1,2,0:T(8,128)}, f32[256,512]{1,0:T(8,128)}, f32[512,512]{1,0:T(8,128)}, f32[512,512]{1,0:T(8,128)}), (f32[3,512,256]{1,2,0:T(8,128)}, f32[256,512]{1,0:T(8,128)}, f32[512,512]{1,0:T(8,128)}, ...) | async-done | bytes 4194320 | tf_op jit(solution)/shard_map/psum | solution.py:213
  361.2 3.1 copy.55
  365.1 1.0 copy.118
  366.1 1.0 copy.119
  (171 shorter events, 15.8 us)
Async XLA Ops:
  7.2 1.1 copy-start
  7.2 48.9 %all-reduce.7.cloned.1.call-start = ((), (), s32[]{:S(2)}) async-start(), calls=%async_computation.1 | async-start | bytes 2097152 | tf_op jit(solution)/shard_map/psum | solution.py:142
  10.6 1.1 copy-start.40
  10.7 1.6 copy-start.27
  18.9 1.2 copy-start.12
  22.9 1.7 copy-start.18
  24.9 0.8 copy-start.19
  28.3 1.7 copy-start.18
  30.3 0.8 copy-start.19
  31.1 24.9 %copy-start.1 = (bf16[1024,512]{1,0:T(8,128)(2,1)S(1)}, bf16[1024,512]{1,0:T(8,128)(2,1)}, u32[]{:S(2)}) copy-start(bf16[1024,512]{1,0:T(8,128)(2,1)} %param.19) | copy-start | bytes 3145732
  31.1 24.9 %copy-start.34 = (f32[512]{0:T(512)S(1)}, f32[512]{0:T(512)}, u32[]{:S(2)}) copy-start(f32[512]{0:T(512)} %param.23) | copy-start | bytes 6148
  33.7 24.8 %copy-start.35 = (f32[512]{0:T(512)S(1)}, f32[512]{0:T(512)}, u32[]{:S(2)}) copy-start(f32[512]{0:T(512)} %param.24) | copy-start | bytes 6148
  33.8 24.8 %copy-start.38 = (f32[512]{0:T(512)S(1)}, f32[512]{0:T(512)}, u32[]{:S(2)}) copy-start(f32[512]{0:T(512)} %param.25) | copy-start | bytes 6148
  33.8 24.8 %copy-start.45 = (f32[512]{0:T(512)S(1)}, f32[512]{0:T(512)}, u32[]{:S(2)}) copy-start(f32[512]{0:T(512)} %param.27) | copy-start | bytes 6148
  33.8 55.2 %all-reduce.9.cloned.1.call-start = ((), (), s32[]{:S(2)}) async-start(), calls=%async_computation.2 | async-start | bytes 2097152 | tf_op jit(solution)/shard_map/psum | solution.py:149
  56.1 1.8 copy-start.4
  56.1 2.5 copy-start.43
  58.5 8.0 %copy-start.41 = (bf16[512,512]{1,0:T(8,128)(2,1)S(1)}, bf16[512,512]{1,0:T(8,128)(2,1)}, u32[]{:S(2)}) copy-start(bf16[512,512]{1,0:T(8,128)(2,1)} %param.28) | copy-start | bytes 1572868
  65.6 1.0 copy-start.46
  66.5 22.5 %copy-start.37 = (f32[512]{0:T(512)S(1)}, f32[512]{0:T(512)}, u32[]{:S(2)}) copy-start(f32[512]{0:T(512)} %param.29) | copy-start | bytes 6148
  68.2 32.6 %all-gather.2.cloned.1.call-start = ((), (), s32[]{:S(2)}) async-start(), calls=%async_computation.3 | async-start | bytes 1572864 | tf_op jit(solution)/shard_map/all_gather | solution.py:159
  69.0 64.9 %all-reduce.11.cloned.1.call-start = ((), (), s32[]{:S(2)}) async-start(), calls=%async_computation.4 | async-start | bytes 2097152 | tf_op jit(solution)/shard_map/psum | solution.py:169
  69.2 31.6 %copy-start.36 = (f32[512]{0:T(512)S(1)}, f32[512]{0:T(512)}, u32[]{:S(2)}) copy-start(f32[512]{0:T(512)} %param.30) | copy-start | bytes 6148
  100.8 3.0 copy-start.10
  100.8 3.0 copy-start.13
  103.8 2.6 copy-start.50
  106.1 4.3 %copy-start.11 = (f32[1024,512]{1,0:T(8,128)}, f32[1024,512]{1,0:T(8,128)S(1)}, u32[]{:S(2)}) copy-start(f32[1024,512]{1,0:T(8,128)S(1)} %get-tuple-element.292) | copy-start | bytes 6291460
  106.1 1.4 copy-start.42
  106.1 2.9 copy-start.49
  106.4 4.1 %copy-start.21 = (bf16[1024,512]{1,0:T(8,128)(2,1)}, bf16[1024,512]{1,0:T(8,128)(2,1)S(1)}, u32[]{:S(2)}) copy-start(bf16[1024,512]{1,0:T(8,128)(2,1)S(1)} %get-tuple-element.283) | copy-start | bytes 3145732
  109.0 2.4 copy-start.44
  110.4 1.0 copy-start.47
  113.1 152.6 %reduce-scatter.2.cloned.1.call-start = ((), (), s32[]{:S(2)}) async-start(), calls=%async_computation.5 | async-start | bytes 1572864 | tf_op jit(solution)/shard_map/reduce_scatter | solution.py:191
  133.9 3.5 copy-start.5
  138.8 2.5 copy-start.26
  140.0 1.3 copy-start.7
  146.1 1.2 copy-start.24
  148.8 1.9 copy-start.25
  150.7 1.4 copy-start.14
  152.1 1.2 copy-start.2
  153.3 0.8 copy-start.15
  154.1 1.0 copy-start.3
  156.6 1.2 copy-start.24
  159.3 1.8 copy-start.25
  161.1 1.4 copy-start.14
  162.5 1.2 copy-start.2
  163.7 0.8 copy-start.15
  164.5 1.0 copy-start.3
  165.5 1.6 copy-start.16
  167.1 3.5 copy-start.29
  168.0 5.6 %copy-start.31 = (bf16[1,1024,256]{2,1,0:T(8,128)(2,1)}, bf16[1,1024,256]{2,1,0:T(8,128)(2,1)S(1)}, u32[]{:S(2)}) copy-start(bf16[1,1024,256]{2,1,0:T(8,128)(2,1)S(1)} %stack_reshape.9) | copy-start | bytes 1572868
  173.6 3.7 copy-start.6
  173.6 187.5 %all-reduce.13.cloned.1.call-start = ((), (), s32[]{:S(2)}) async-start(), calls=%async_computation.6 | async-start | bytes 8388608 | tf_op jit(solution)/shard_map/psum | solution.py:213
  173.9 3.4 copy-start.48
  177.3 2.1 copy-start.8
  177.3 2.1 copy-start.20
  179.4 1.3 copy-start.30
  179.4 1.3 copy-start.32
  179.4 1.4 copy-start.33
  183.0 3.0 copy-start.17
  183.0 82.7 %copy-start.9 = (f32[1024,512]{1,0:T(8,128)S(1)}, f32[1024,512]{1,0:T(8,128)}, u32[]{:S(2)}) copy-start(f32[1024,512]{1,0:T(8,128)} %copy-done.7) | copy-start | bytes 6291460
  361.2 3.1 copy-start.28
  361.2 3.9 %copy-start.23 = (f32[512,512]{1,0:T(8,128)S(1)}, f32[512,512]{1,0:T(8,128)}, u32[]{:S(2)}) copy-start(f32[512,512]{1,0:T(8,128)} %get-tuple-element.508) | copy-start | bytes 3145732
  364.3 1.8 copy-start.22
  (1 other events, 0.7 us)
Sparse Core Ops, SparseCore 0:
  33.9 22.1 all-reduce.6
  68.3 20.6 all-reduce.8
  90.5 10.2 all-gather.1
  113.3 20.5 all-reduce.10
  173.7 9.5 reduce-scatter.1
  190.3 170.8 all-reduce.12
where the time goes:
time: 375 us; the launch traced here: 374 us
  waiting for transfers between devices  165 us (44%)
  blocking collectives  79.6 us (21%)
  matrix products  46.4 us (12%)
  local copies, waits for them, and re-layouts  34.9 us (9%)
  other arithmetic  32.5 us (9%)
  between operations  14.6 us (4%)
    psum x1, waiting for transfers between devices, on_device(): lax.psum((grad_w_qkv, grad_b_qv, grad_w_out, grad_b_out, grad_norm1_gain,...  93.5 us
    psum x1, blocking collectives, on_device(): lax.psum((grad_w_qkv, grad_b_qv, grad_w_out, grad_b_out, grad_norm1_gain,...  79.6 us
    psum x1, waiting for transfers between devices, on_device(): lax.psum(attn_partial.astype(jnp.bfloat16), 'tensor').astype(jnp.float32)  22.2 us
    psum x1, waiting for transfers between devices, on_device(): lax.psum(ffn_partial.astype(jnp.bfloat16), 'tensor').astype(jnp.float32)  20.7 us
    psum x1, waiting for transfers between devices, on_device(): lax.psum(jnp.dot(act_low, w_down, preferred_element_type=jnp.float32).ast...  19.8 us
    unnamed x91, local copies, waits for them, and re-layouts  15.2 us
    all_gather x1, waiting for transfers between devices, on_device(): lax.all_gather(d_out, 'tensor', axis=0, tiled=True).astype(jnp.float32)  8.04 us
    reduce_sum x3, other arithmetic, layer_norm(): return centred * lax.rsqrt(spread + NORM_EPSILON) * norm_gain + norm_shift  7.84 us
  transfers between devices with their start and end apart: 6, of which 5 were waited for; matrix products, arithmetic and copies ran while one was open for 5% of the time, Pallas kernels for 0%

commit v1 on v0

v1 whole, which is shorter than its diff:
```python
import jax
import jax.numpy as jnp
from jax import lax
from jax.experimental import pallas as pl
from jax.experimental.pallas import tpu as pltpu
from jax.sharding import PartitionSpec as P

HD = 128
NORM_EPSILON = 1e-05
MASKED_SCORE = -1e30
LOG2E = 1.4426950408889634
F32 = jnp.float32
BF16 = jnp.bfloat16
MESH = pl.DeviceIdType.MESH


def nn(a, b):
    return lax.dot_general(a, b, (((1,), (0,)), ((), ())), preferred_element_type=F32)


def nt(a, b):
    return lax.dot_general(a, b, (((1,), (1,)), ((), ())), preferred_element_type=F32)


def tn(a, b):
    return lax.dot_general(a, b, (((0,), (0,)), ((), ())), preferred_element_type=F32)


def torus_sizes(chips):
    side = 1
    for k in range(1, chips + 1):
        if chips % (k * k) == 0 and chips // (k * k) >= k:
            side = k
    return side, side, chips // (side * side)


class Semaphores:
    def __init__(self):
        self.count = 0

    def take(self, n=1):
        first = self.count
        self.count += n
        return first


class Stage:
    def __init__(self, size, place, peer, sems, send_sem, recv_sem):
        self.size, self.place, self.peer = size, place, peer
        self.first = sems.take(size - 1)
        self.send_sem, self.recv_sem = send_sem, recv_sem

    def to(self, j):
        return lax.rem(self.place + j, self.size)

    def copy(self, j, src, dst):
        slot = self.first + j - 1
        return pltpu.make_async_remote_copy(
            src_ref=src,
            dst_ref=dst,
            send_sem=self.send_sem.at[slot],
            recv_sem=self.recv_sem.at[slot],
            device_id=self.peer(self.to(j)),
            device_id_type=MESH,
        )


def blk(start, size, align=None):
    return pl.ds(pl.multiple_of(start, align or size), size)


class Reduction:
    def __init__(self, rows, axes, sems, send_sem, recv_sem):
        (n1, m1, peer1), (n2, m2, peer2), (n3, m3, peer3) = axes
        self.rows = rows
        self.p1, self.p2 = rows // n1, rows // (n1 * n2)
        self.split_z = (self.p2 // n3) % 16 == 0 and self.p2 % n3 == 0
        self.p3 = self.p2 // n3 if self.split_z else self.p2
        self.n1, self.n2, self.n3 = n1, n2, n3
        self.m1, self.m2, self.m3 = m1, m2, m3
        make = lambda n, m, peer: Stage(n, m, peer, sems, send_sem, recv_sem)
        self.s1, self.s2, self.s3 = make(n1, m1, peer1), make(n2, m2, peer2), make(n3, m3, peer3)
        self.g1, self.g2 = make(n1, m1, peer1), make(n2, m2, peer2)
        self.g3 = make(n3, m3, peer3) if self.split_z else None

    @staticmethod
    def scratch(rows, cols, sizes):
        n1, n2, n3 = sizes
        p1, p2 = rows // n1, rows // (n1 * n2)
        split_z = (p2 // n3) % 16 == 0 and p2 % n3 == 0
        p3 = p2 // n3 if split_z else p2
        return [
            pltpu.VMEM((n1 - 1, p1, cols), BF16),
            pltpu.VMEM((p1, cols), BF16),
            pltpu.VMEM((n2 - 1, p2, cols), BF16),
            pltpu.VMEM((p2, cols), BF16),
            pltpu.VMEM((n3 - 1, p3, cols), BF16),
        ]

    def bind(self, grad, scratch, out):
        self.grad, self.out = grad, out
        self.r1, self.t1, self.r2, self.t2, self.r3 = scratch
        self.off1 = pl.multiple_of(self.m1 * self.p1, self.p1)
        self.off2 = pl.multiple_of(self.off1 + self.m2 * self.p2, self.p2)
        self.off3 = self.off2
        if self.split_z:
            self.off3 = pl.multiple_of(self.off2 + self.m3 * self.p3, self.p3)

    def sends(self, name):
        if name == "s1":
            return [self.s1.copy(j, self.grad.at[blk(self.s1.to(j) * self.p1, self.p1)], self.r1.at[j - 1]) for j in range(1, self.n1)]
        if name == "s2":
            return [self.s2.copy(j, self.t1.at[blk(self.s2.to(j) * self.p2, self.p2)], self.r2.at[j - 1]) for j in range(1, self.n2)]
        if name == "s3":
            if self.split_z:
                return [self.s3.copy(j, self.t2.at[blk(self.s3.to(j) * self.p3, self.p3)], self.r3.at[j - 1]) for j in range(1, self.n3)]
            return [self.s3.copy(j, self.t2, self.r3.at[j - 1]) for j in range(1, self.n3)]
        if name == "g3":
            if not self.split_z:
                return []
            piece = self.out.at[pl.ds(self.off3, self.p3)]
            return [self.g3.copy(j, piece, piece) for j in range(1, self.n3)]
        if name == "g2":
            piece = self.out.at[pl.ds(self.off2, self.p2)]
            return [self.g2.copy(j, piece, piece) for j in range(1, self.n2)]
        piece = self.out.at[pl.ds(self.off1, self.p1)]
        return [self.g1.copy(j, piece, piece) for j in range(1, self.n1)]

    def landed(self, name):
        if name not in ("g1", "g2", "g3"):
            return self.sends(name)
        if name == "g3" and not self.split_z:
            return []
        stage, base, size, n = {
            "g3": (self.g3, self.off2, self.p3, self.n3),
            "g2": (self.g2, self.off1, self.p2, self.n2),
            "g1": (self.g1, 0, self.p1, self.n1),
        }[name]
        found = []
        for j in range(1, n):
            sender = lax.rem(stage.place + n - j, n)
            piece = self.out.at[pl.ds(pl.multiple_of(base + sender * size, size), size)]
            found.append(stage.copy(j, piece, piece))
        return found

    def start(self, name):
        for c in self.sends(name):
            c.start()

    def arrive(self, name):
        for c in self.landed(name):
            c.wait_recv()

    def drain(self):
        for name in ("s1", "s2", "s3", "g3", "g2", "g1"):
            for c in self.sends(name):
                c.wait_send()

    def step(self, number):
        if number == 0:
            self.start("s1")
        elif number == 1:
            self.arrive("s1")
            total = self.grad[blk(self.m1 * self.p1, self.p1), :].astype(F32)
            for j in range(self.n1 - 1):
                total = total + self.r1[j].astype(F32)
            self.t1[...] = total.astype(BF16)
            self.start("s2")
        elif number == 2:
            self.arrive("s2")
            total = self.t1[blk(self.m2 * self.p2, self.p2), :].astype(F32)
            for j in range(self.n2 - 1):
                total = total + self.r2[j].astype(F32)
            self.t2[...] = total.astype(BF16)
            self.start("s3")
        elif number == 3:
            self.arrive("s3")
            if self.split_z:
                total = self.t2[blk(self.m3 * self.p3, self.p3), :].astype(F32)
            else:
                total = self.t2[...].astype(F32)
            for j in range(self.n3 - 1):
                total = total + self.r3[j].astype(F32)
            self.out[pl.ds(self.off3, self.p3), :] = total.astype(BF16)
            self.start("g3")
        elif number == 4:
            self.arrive("g3")
            self.start("g2")
        elif number == 5:
            self.arrive("g2")
            self.start("g1")
        else:
            self.arrive("g1")


def make_kernel(sizes, length, width, hidden_units):
    nx, ny, nz = sizes
    half = length // 2
    qb = 256
    fh = hidden_units // 2
    heads = 2
    hw = heads * HD
    kcat = 3 * HD
    score_c = HD ** (-0.5) * LOG2E
    key_rows = 512

    grads = (("a", fh, width), ("b", width, fh), ("c", hw, width), ("d0", width, kcat), ("d1", width, kcat))

    scratch = dict(
        xt=pltpu.VMEM((width, length), BF16),
        q=pltpu.VMEM((heads, length, HD), BF16),
        k=pltpu.VMEM((heads, length, HD), BF16),
        v=pltpu.VMEM((heads, length, HD), BF16),
        kt=pltpu.VMEM((heads, HD, length), BF16),
        vt=pltpu.VMEM((heads, HD, length), BF16),
        segf=pltpu.VMEM((1, length), F32),
        kb=pltpu.VMEM((length, qb), F32),
        lse=pltpu.VMEM((heads, 1, length), F32),
        mix=pltpu.VMEM((heads, length, HD), BF16),
        mo=pltpu.VMEM((heads, half, HD), BF16),
        wout_o=pltpu.VMEM((hw, width), BF16),
        win_o=pltpu.VMEM((width, fh), BF16),
        wdown_o=pltpu.VMEM((fh, width), BF16),
        bin_o=pltpu.VMEM((1, fh), F32),
        hid=pltpu.VMEM((half, width), BF16),
        act=pltpu.VMEM((2, half, fh), BF16),
        gp=pltpu.VMEM((2, qb, fh), F32),
        ddown=pltpu.VMEM((half, width), BF16),
        dup=pltpu.VMEM((2, half, fh), BF16),
        dattn=pltpu.VMEM((half, width), BF16),
        dpre=pltpu.VMEM((half, width), F32),
        dmix=pltpu.VMEM((heads, length, HD), BF16),
        dmo=pltpu.VMEM((heads, half, HD), BF16),
        dkacc=pltpu.VMEM((heads, length, HD), F32),
        dvacc=pltpu.VMEM((heads, length, HD), F32),
        dcat=pltpu.VMEM((heads, length, kcat), BF16),
        dxs=pltpu.VMEM((half, width), BF16),
        dxr=pltpu.VMEM((half, width), BF16),
        sm=pltpu.VMEM((16, width), F32),
        smt=pltpu.VMEM((16, width), F32),
        sm0=pltpu.VMEM((16, width), F32),
        sm1=pltpu.VMEM((16, width), F32),
        sm2=pltpu.VMEM((16, width), F32),
        smr1=pltpu.VMEM((nx - 1, 16, width), F32),
        smr2=pltpu.VMEM((ny - 1, 16, width), F32),
        smr3=pltpu.VMEM((nz - 1, 16, width), F32),
    )
    for name, rows, cols in grads:
        scratch["g_" + name] = pltpu.VMEM((rows, cols), BF16)
        if name in "abc":
            scratch["gs_" + name] = pltpu.VMEM((rows, cols), BF16)
            scratch["gr_" + name] = pltpu.VMEM((rows, cols), BF16)
        for i, spec in enumerate(Reduction.scratch(rows, cols, sizes)):
            scratch[f"red_{name}_{i}"] = spec

    names = list(scratch)
    n_sems = 256

    def kernel(x, wqkv, bqv, wout, bout, n1g, n1s, win, bin_, wdown, bdown, n2g, n2s, seg, dout, *rest):
        out_o, din_o, ga_o, gb_o, gc_o, gd0_o, gd1_o, small_o = rest[:8]
        refs = dict(zip(names, rest[8 : 8 + len(names)]))
        send_sem, recv_sem = rest[8 + len(names) :]
        s = type("Scratch", (), refs)
        sems = Semaphores()

        dp = lax.axis_index("dp")
        t = lax.axis_index("tensor")
        other = 1 - t
        xi = lax.rem(dp, nx)
        yi = lax.rem(lax.div(dp, nx), ny)
        zi = lax.div(dp, nx * ny)
        m1 = xi + t * (yi - xi)
        m2 = yi + t * (xi - yi)
        stride1 = 1 + t * (nx - 1)
        stride2 = nx + t * (1 - nx)
        peer1 = lambda c: (dp + (c - m1) * stride1, t)
        peer2 = lambda c: (dp + (c - m2) * stride2, t)
        peer3 = lambda c: (dp + (c - zi) * (nx * ny), t)
        axes = ((nx, m1, peer1), (ny, m2, peer2), (nz, zi, peer3))

        barrier = pltpu.get_barrier_semaphore()
        pl.semaphore_signal(barrier, inc=1, device_id=(dp, other), device_id_type=MESH)
        for n, m, peer in axes:
            for j in range(1, n):
                pl.semaphore_signal(barrier, inc=1, device_id=peer(lax.rem(m + j, n)), device_id_type=MESH)
        pl.semaphore_wait(barrier, 1 + (nx - 1) + (ny - 1) + (nz - 1))

        def across(src, dst, slot=None):
            slot = sems.take() if slot is None else slot
            return pltpu.make_async_remote_copy(
                src_ref=src, dst_ref=dst, send_sem=send_sem.at[slot], recv_sem=recv_sem.at[slot],
                device_id=(dp, other), device_id_type=MESH,
            )

        my0 = pl.multiple_of(t * half, half)
        ot0 = pl.multiple_of(other * half, half)
        all_copies = []

        def launch(*copies):
            for c in copies:
                c.start()
                all_copies.append(c)

        weights = [
            across(wout, s.wout_o),
            across(win, s.win_o),
            across(wdown, s.wdown_o),
            across(bin_, s.bin_o),
        ]
        launch(*weights)

        mix_out = [across(s.mix.at[h, pl.ds(ot0, half)], s.mo.at[h]) for h in range(heads)]
        dmix_slots = [sems.take() for _ in range(heads)]
        dmix_out = [across(s.dmo.at[h], s.dmix.at[h, pl.ds(my0, half)], dmix_slots[h]) for h in range(heads)]
        dmix_in = [across(s.dmo.at[h], s.dmix.at[h, pl.ds(ot0, half)], dmix_slots[h]) for h in range(heads)]
        part = {name: across(refs["gs_" + name], refs["gr_" + name]) for name in "abc"}
        dx_out = across(s.dxs, s.dxr)
        small_t = across(s.sm, s.smt)
        red = {}
        outs = dict(a=ga_o, b=gb_o, c=gc_o, d0=gd0_o, d1=gd1_o)
        for name, rows, cols in grads:
            red[name] = Reduction(rows, axes, sems, send_sem, recv_sem)
            red[name].bind(refs["g_" + name], [refs[f"red_{name}_{i}"] for i in range(5)], outs[name])
        small_stages = [Stage(n, m, peer, sems, send_sem, recv_sem) for n, m, peer in axes]
        small_bufs = [(s.sm0, s.smr1), (s.sm1, s.smr2), (s.sm2, s.smr3)]

        def small_copies(i):
            src, dst = small_bufs[i]
            return [small_stages[i].copy(j, src, dst.at[j - 1]) for j in range(1, axes[i][0])]

        assert sems.count <= n_sems

        segf = seg[...].astype(F32)
        s.segf[...] = segf
        for b in range(length // 128):
            rows = jnp.broadcast_to(s.segf[:, b * 128 : (b + 1) * 128], (128, 128)).T
            for c in range(qb // 128):
                s.kb[b * 128 : (b + 1) * 128, c * 128 : (c + 1) * 128] = rows

        def project(i, _):
            rows = blk(i * qb, qb)
            xb = x[rows, :]
            s.xt[:, rows] = xb.T
            qv = nn(xb, wqkv[0]) + bqv[0:1, :]
            kv = nn(xb, wqkv[1])
            vv = nn(xb, wqkv[2]) + bqv[1:2, :]
            ql, kl, vl = qv.astype(BF16), kv.astype(BF16), vv.astype(BF16)
            for h in range(heads):
                cols = slice(h * HD, (h + 1) * HD)
                s.q[h, rows, :] = ql[:, cols]
                s.k[h, rows, :] = kl[:, cols]
                s.v[h, rows, :] = vl[:, cols]
                s.kt[h, :, rows] = kl[:, cols].T
                s.vt[h, :, rows] = vl[:, cols].T
            return 0

        lax.fori_loop(0, length // qb, project, 0)

        def block_scores(h, rows):
            products = nt(s.k[h], s.q[h, rows, :]) * score_c
            return jnp.where(s.kb[...] == s.segf[:, rows], products, MASKED_SCORE)

        blocks = length // qb

        def attend(i, _):
            h = lax.rem(i, heads)
            qi = lax.rem(other * (blocks // 2) + lax.div(i, heads), blocks)
            rows = blk(qi * qb, qb)
            scores = block_scores(h, rows)
            top = jnp.max(scores, 0, keepdims=True)
            weights_t = jnp.exp2(scores - top)
            total = jnp.sum(weights_t, 0, keepdims=True)
            mixed = nn(s.vt[h], weights_t.astype(BF16)) * (1.0 / total)
            s.mix[h, rows, :] = mixed.T.astype(BF16)
            s.lse[h, :, rows] = top + jnp.log2(total)
            return 0

        n_att = heads * blocks
        lax.fori_loop(0, n_att // 2, attend, 0)
        launch(*mix_out)
        lax.fori_loop(n_att // 2, n_att, attend, 0)
        for c in weights + mix_out:
            c.wait_recv()

        s.sm[...] = jnp.zeros_like(s.sm)

        def add_small(row, value):
            s.sm[row : row + 1, :] += value

        def row_sum(value):
            return jnp.sum(value, 0, keepdims=True)

        def norm(v):
            average = jnp.mean(v, -1, keepdims=True)
            centred = v - average
            rs = lax.rsqrt(jnp.mean(centred * centred, -1, keepdims=True) + NORM_EPSILON)
            return centred * rs, rs

        def norm_back(e, n, rs):
            return (e - jnp.mean(e, -1, keepdims=True) - n * jnp.mean(e * n, -1, keepdims=True)) * rs

        halves = ((win, bin_, wdown, wout), (s.win_o, s.bin_o, s.wdown_o, s.wout_o))

        def middle(r, _):
            here = blk(r * qb, qb)
            whole = pl.ds(pl.multiple_of(my0 + r * qb, qb), qb)
            mine = jnp.concatenate([s.mix[h, whole, :] for h in range(heads)], 1)
            theirs = jnp.concatenate([s.mo[h, here, :] for h in range(heads)], 1)
            pre1 = x[whole, :].astype(F32) + (nn(mine, wout[...]) + nn(theirs, s.wout_o[...]) + bout[...])
            n1, rs1 = norm(pre1)
            hidden = n1 * n1g[...] + n1s[...]
            low = hidden.astype(BF16)
            s.hid[here, :] = low
            for f, (w_in, b_in, _, _) in enumerate(halves):
                up = nn(low, w_in[...]) + b_in[...]
                cdf = 0.5 * (1.0 + lax.erf(up * (0.5**0.5)))
                s.act[f, here, :] = (up * cdf).astype(BF16)
                s.gp[f] = cdf + up * (jnp.exp2(up * up * (-0.5 * LOG2E)) * 0.3989422804014327)
            down = nn(s.act[0, here, :], wdown[...]) + nn(s.act[1, here, :], s.wdown_o[...]) + bdown[...]
            n2, rs2 = norm(hidden + down)
            row_mask = (s.kb[whole, 0:1] != 0.0).astype(F32)
            out_o[here, :] = ((n2 * n2g[...] + n2s[...]) * row_mask).astype(BF16)
            cot = dout[here, :].astype(F32) * row_mask
            add_small(0, row_sum(cot))
            add_small(1, row_sum(cot * n2))
            d_resid = norm_back(cot * n2g[...], n2, rs2)
            d_down = d_resid.astype(BF16)
            s.ddown[here, :] = d_down
            add_small(2, row_sum(d_down.astype(F32)))
            d_hidden = d_resid
            for f, (w_in, _, w_down, _) in enumerate(halves):
                d_up = (nt(d_down, w_down[...]) * s.gp[f]).astype(BF16)
                s.dup[f, here, :] = d_up
                add_small(3 + f, row_sum(d_up.astype(F32)))
                d_hidden = d_hidden + nt(d_up, w_in[...])
            add_small(5, row_sum(d_hidden))
            add_small(6, row_sum(d_hidden * n1))
            d_pre = norm_back(d_hidden * n1g[...], n1, rs1)
            s.dpre[here, :] = d_pre
            d_attn = d_pre.astype(BF16)
            s.dattn[here, :] = d_attn
            add_small(7, row_sum(d_attn.astype(F32)))
            dm = nt(d_attn, wout[...]).astype(BF16)
            do = nt(d_attn, s.wout_o[...]).astype(BF16)
            for h in range(heads):
                s.dmix[h, whole, :] = dm[:, h * HD : (h + 1) * HD]
                s.dmo[h, here, :] = do[:, h * HD : (h + 1) * HD]
            return 0

        lax.fori_loop(0, half // qb, middle, 0)
        launch(*dmix_out)

        def grad_block(dst, lhs, rhs):
            n = lhs.shape[1]

            def body(i, _):
                cols = blk(i * qb, qb)
                dst[cols, :] = tn(lhs[:, cols], rhs[...]).astype(BF16)
                return 0

            lax.fori_loop(0, n // qb, body, 0)

        grad_block(s.gs_a, s.act.at[1], s.ddown)
        launch(part["a"])
        grad_block(s.g_a, s.act.at[0], s.ddown)
        grad_block(s.gs_b, s.hid, s.dup.at[1])
        launch(part["b"])

        def join(name):
            part[name].wait_recv()
            mine, theirs = refs["g_" + name], refs["gr_" + name]
            mine[...] = (mine[...].astype(F32) + theirs[...].astype(F32)).astype(BF16)
            red[name].step(0)

        join("a")
        grad_block(s.g_b, s.hid, s.dup.at[0])
        theirs = jnp.concatenate([s.mo[h] for h in range(heads)], 1)
        s.gs_c[...] = tn(theirs, s.dattn[...]).astype(BF16)
        launch(part["c"])
        join("b")
        mine = jnp.concatenate([s.mix[h, pl.ds(my0, half), :] for h in range(heads)], 1)
        s.g_c[...] = tn(mine, s.dattn[...]).astype(BF16)
        join("c")

        s.dkacc[...] = jnp.zeros_like(s.dkacc)
        s.dvacc[...] = jnp.zeros_like(s.dvacc)
        for c in dmix_in:
            c.wait_recv()

        def finish_head(h):
            dk = (s.dkacc[h] * (HD ** (-0.5))).astype(BF16)
            dv = s.dvacc[h].astype(BF16)
            s.dcat[h, :, HD : 2 * HD] = dk
            s.dcat[h, :, 2 * HD :] = dv
            s.sm[8:9, h * HD : (h + 1) * HD] = row_sum(s.dcat[h, :, 0:HD].astype(F32))
            s.sm[8:9, hw + h * HD : hw + (h + 1) * HD] = row_sum(dv.astype(F32))
            dst = s.g_d0 if h == 0 else s.g_d1

            def body(i, _):
                rows = blk(i * 128, 128)
                dst[rows, :] = nn(s.xt[rows, :], s.dcat[h]).astype(BF16)
                return 0

            lax.fori_loop(0, width // 128, body, 0)
            red["d0" if h == 0 else "d1"].step(0)

        def attend_back(i, _):
            h = lax.div(i, blocks)
            qi = lax.rem(t * (blocks // 2) + lax.rem(i, blocks), blocks)
            rows = blk(qi * qb, qb)
            d_mixed = s.dmix[h, rows, :]
            delta = row_sum((d_mixed.astype(F32) * s.mix[h, rows, :].astype(F32)).T)
            probs = jnp.exp2(block_scores(h, rows) - s.lse[h, :, rows])
            low = probs.astype(BF16)
            s.dvacc[h] += nn(low, d_mixed)
            d_scores = (probs * (nt(s.v[h], d_mixed) - delta)).astype(BF16)
            s.dkacc[h] += nn(d_scores, s.q[h, rows, :])
            dqt = nn(s.kt[h], d_scores) * (HD ** (-0.5))
            s.dcat[h, rows, 0:HD] = dqt.T.astype(BF16)

            @pl.when(i == blocks - 1)
            def _():
                finish_head(0)
                red["a"].step(1)

            @pl.when(i == blocks + 1)
            def _():
                red["b"].step(1)

            @pl.when(i == blocks + 2)
            def _():
                red["a"].step(2)
                red["c"].step(1)

            return 0

        lax.fori_loop(0, n_att, attend_back, 0)
        finish_head(1)
        launch(small_t)
        red["b"].step(2)
        red["d0"].step(1)
        red["c"].step(2)
        red["a"].step(3)
        small_t.wait_recv()
        s.sm0[...] = s.sm[...] + s.smt[...]
        s.sm0[3:4, :] = s.sm[3:4, :] + s.smt[4:5, :]
        s.sm0[8:9, :] = s.sm[8:9, :]
        for c in small_copies(0):
            c.start()

        def project_back(i, _):
            rows = blk(lax.rem(other * (blocks // 2) + i, blocks) * qb, qb)
            wide = jnp.concatenate([s.dcat[h, rows, :] for h in range(heads)], 1)
            wcat = jnp.concatenate(
                [wqkv[c][:, h * HD : (h + 1) * HD] for h in range(heads) for c in range(3)], 1
            )
            return nt(wide, wcat)

        def send_rows(i, _):
            s.dxs[blk(i * qb, qb), :] = project_back(i, 0).astype(BF16)
            return 0

        def keep_rows(i, _):
            s.dpre[blk((i - blocks // 2) * qb, qb), :] += project_back(i, 0)
            return 0

        lax.fori_loop(0, blocks // 2, send_rows, 0)
        launch(dx_out)
        red["b"].step(3)
        red["d0"].step(2)
        red["d1"].step(1)
        red["c"].step(3)
        lax.fori_loop(blocks // 2, blocks, keep_rows, 0)
        red["a"].step(4)
        red["b"].step(4)
        dx_out.wait_recv()
        din_o[...] = (s.dpre[...] + s.dxr[...].astype(F32)).astype(BF16)

        def small_sum(i):
            src, got = small_bufs[i]
            for c in small_copies(i):
                c.wait_recv()
            total = src[...]
            for j in range(axes[i][0] - 1):
                total = total + got[j]
            return total

        red["d1"].step(2)
        s.sm1[...] = small_sum(0)
        for c in small_copies(1):
            c.start()
        red["d0"].step(3)
        red["a"].step(5)
        red["c"].step(4)
        red["b"].step(5)
        red["d1"].step(3)
        s.sm2[...] = small_sum(1)
        for c in small_copies(2):
            c.start()
        red["d0"].step(4)
        red["c"].step(5)
        red["d0"].step(5)
        red["d1"].step(4)
        small_o[...] = small_sum(2)
        red["a"].step(6)
        red["d1"].step(5)
        red["b"].step(6)
        red["c"].step(6)
        red["d0"].step(6)
        red["d1"].step(6)
        for c in all_copies:
            c.wait_send()
        for i in range(3):
            for c in small_copies(i):
                c.wait_send()
        for r in red.values():
            r.drain()

    return kernel, list(scratch.values()), n_sems, grads


def solution(mesh):
    chips = mesh.shape["dp"]
    sizes = torus_sizes(chips)

    def on_device(
        inputs, w_qkv, b_qv, w_out, b_out, norm1_gain, norm1_shift, w_in, b_in, w_down, b_down, norm2_gain, norm2_shift,
        segment_ids, d_out,
    ):
        length, width = inputs.shape
        fh = w_in.shape[1]
        hw = w_out.shape[0]
        kernel, scratch, n_sems, grads = make_kernel(sizes, length, width, 2 * fh)
        row = lambda v: v.reshape(1, -1)
        vmem = pl.BlockSpec(memory_space=pltpu.VMEM)
        half = length // 2
        shapes = [
            jax.ShapeDtypeStruct((half, width), BF16),
            jax.ShapeDtypeStruct((half, width), BF16),
            *[jax.ShapeDtypeStruct((rows, cols), BF16) for _, rows, cols in grads],
            jax.ShapeDtypeStruct((16, width), F32),
        ]
        output, d_inputs, ga, gb, gc, gd0, gd1, small = pl.pallas_call(
            kernel,
            out_shape=shapes,
            in_specs=[vmem] * 15,
            out_specs=[vmem] * len(shapes),
            scratch_shapes=[*scratch, pltpu.SemaphoreType.DMA((n_sems,)), pltpu.SemaphoreType.DMA((n_sems,))],
            compiler_params=pltpu.CompilerParams(
                collective_id=0, has_side_effects=True, vmem_limit_bytes=60 * 1024 * 1024
            ),
        )(
            inputs, w_qkv, b_qv, w_out, row(b_out), row(norm1_gain), row(norm1_shift), w_in, row(b_in), w_down,
            row(b_down), row(norm2_gain), row(norm2_shift), segment_ids, d_out,
        )
        grad_w_qkv = jnp.stack(
            [jnp.concatenate([g[:, c * HD : (c + 1) * HD] for g in (gd0, gd1)], 1) for c in range(3)]
        ).astype(F32)
        return (
            output,
            d_inputs,
            grad_w_qkv,
            small[8].reshape(2, hw),
            gc.astype(F32),
            small[7],
            small[6],
            small[5],
            gb.astype(F32),
            small[3],
            ga.astype(F32),
            small[2],
            small[1],
            small[0],
        )

    placed = (
        P("dp", None),
        P(None, None, "tensor"),
        P(None, "tensor"),
        P("tensor", None),
        P(),
        P(),
        P(),
        P(None, "tensor"),
        P("tensor"),
        P("tensor", None),
        P(),
        P(),
        P(),
        P("dp", None),
        P(("dp", "tensor"), None),
    )
    return jax.shard_map(
        on_device,
        mesh=mesh,
        in_specs=placed,
        out_specs=(
            P(("dp", "tensor"), None),
            P(("dp", "tensor"), None),
            P(None, None, "tensor"),
            P(None, "tensor"),
            P("tensor", None),
            P(),
            P(),
            P(),
            P(None, "tensor"),
            P("tensor"),
            P("tensor", None),
            P(),
            P(),
            P(),
        ),
        check_vma=False,
    )
```

time: 375 us -> 92.9 us (0.25)
  waiting for transfers between devices: 165 us -> 0 us
  Pallas kernels: 0 us -> 81.6 us
  blocking collectives: 79.6 us -> 0 us
  matrix products: 46.4 us -> 0 us
  local copies, waits for them, and re-layouts: 34.9 us -> 5.04 us
  other arithmetic: 32.5 us -> 5.37 us
  between operations: 14.6 us -> 0.71 us
    psum x4 -> x0, waiting for transfers between devices: 156 us -> none  [the longest x1 93.5 us: on_device(): lax.psum((grad_w_qkv, grad_b_qv, grad_w_out, grad_b_out, grad_norm1_gain,...]
    pallas_call x0 -> x1, Pallas kernels: none -> 81.6 us  [on_device(): pl.pallas_call(kernel, out_shape=shapes, in_specs=[vmem] * 15, out_specs=...]
    psum x1 -> x0, blocking collectives: 79.6 us -> none  [on_device(): lax.psum((grad_w_qkv, grad_b_qv, grad_w_out, grad_b_out, grad_norm1_gain,...]
    dot_general x26 -> x0, matrix products: 46.4 us -> none  [the longest x1 7 us: feed_forward(): jnp.dot(hidden_low, w_in, preferred_element_type=jnp.float32) + b_in]
    reduce_sum x13 -> x0, other arithmetic: 21.8 us -> none  [the longest x3 7.84 us: layer_norm(): return centred * lax.rsqrt(spread + NORM_EPSILON) * norm_gain + norm_shift]
    unnamed x91 -> x10, local copies, waits for them, and re-layouts: 15.2 us -> 1.6 us
    all_gather x1 -> x0, waiting for transfers between devices: 8.04 us -> none  [on_device(): lax.all_gather(d_out, 'tensor', axis=0, tiled=True).astype(jnp.float32)]
    while x34 -> x0, local copies, waits for them, and re-layouts: 6.38 us -> none
  transfers between devices with their start and end apart: 6 -> 0, of which waited for: 5 -> 0; matrix products, arithmetic and copies ran while one was open for 5% -> 0% of each run, Pallas kernels for 0% -> 0%
where the time goes in v1:
time: 92.9 us; the launch traced here: 92.7 us
  Pallas kernels  81.6 us (88%)
  other arithmetic  5.37 us (6%)
  local copies, waits for them, and re-layouts  5.04 us (5%)
    pallas_call x1, Pallas kernels, on_device(): pl.pallas_call(kernel, out_shape=shapes, in_specs=[vmem] * 15, out_specs=...  81.6 us

profile of v1, /device:TPU:0, one launch (start us, length us, event | category | flops | bytes accessed | tf_op | source)
XLA Modules:
  0.0 92.7 jit_solution(14053773124906679135)
XLA Ops:
  0.7 81.6 %shard_map.254 = (bf16[512,512]{1,0:T(8,128)(2,1)}, bf16[512,512]{1,0:T(8,128)(2,1)}, bf16[512,512]{1,0:T(8,128)(2,1)}, bf16[512,512]{1,0:T(8,128)(2,1)}, bf16[2...) custom-call(bf16[1024,512]{1,0:T(8,128)(2,1)} %x.1, ...), custom_call_target="tpu_custom_call" | custom-call | tf_op jit(solution)/shard_map/pallas_call | solution.py:643
  82.2 1.6 %fusion.2 = (f32[1,512]{1,0:T(1,128)}, f32[1,512]{1,0:T(1,128)}, f32[1,512]{1,0:T(1,128)}, f32[1,512]{1,0:T(1,128)}, f32[1,512]{1,0:T(1,128)}, /*index=5*/f32[1,512]{1,0:T(1,128)}, f32[1,512]{1,0:T(1,128)}, f32[512]{0:T(512)S(1)}) fusion(f32[16,512]{1,0:T(8,128)} %get-tuple-element.26), kind=kLoop, calls=%fused_computation.7 | loop fusion | bytes 32768 | tf_op jit(solution)/shard_map/slice | solution.py:673
  83.8 0.6 reshape_squeeze.3
  84.4 1.8 %convert_element_type.13 = f32[256,512]{1,0:T(8,128)} convert(bf16[256,512]{1,0:T(8,128)(2,1)} %get-tuple-element.27) | non-fusion elementwise | flops 131072 | bytes 786432 | tf_op jit(solution)/shard_map/convert_element_type | solution.py:664
  86.2 1.3 %fusion = (bf16[512,128]{1,0:T(8,128)(2,1)S(1)}, bf16[512,128]{1,0:T(8,128)(2,1)S(1)}, bf16[512,128]{1,0:T(8,128)(2,1)S(1)}, bf16[512,128]{1,0:T(8,128)(2,1)S(1)...) fusion(bf16[512,384]{1,0:T(8,128)(2,1)} %get-tuple-element.24, bf16[512,384]{1,0:T(8,128)(2,1)} %get-tuple-element.25), kind=kLoop, calls=%fused_computation.5 | loop fusion | bytes 1572864 | tf_op jit(solution)/shard_map/slice | solution.py:657
  87.5 0.0 copy-start.1
  87.6 0.0 copy-start
  87.6 1.3 %maximum_convert_fusion = f32[3,512,256]{2,1,0:T(8,128)} fusion(bf16[1,512,256]{2,1,0:T(8,128)(2,1)S(1)} %maximum_bitcast_fusion.2, bf16[1,512,256]{2,1,0:T(8,128)(2,1)S(1)} %maximum_bitcast_fusion.1, bf16[1,512,256]{2,1,0:T(8,128)(2,1)S(1)} %maximum_bitcast_fusion), kind=kLoop, calls=%fused_computation | loop fusion | flops 1179648 | bytes 2359296 | tf_op jit(solution)/shard_map/convert_element_type | solution.py:658
  88.9 0.0 copy-done.1
  88.9 0.0 copy-start.3
  88.9 1.1 %convert_element_type.14 = f32[512,512]{1,0:T(8,128)} convert(bf16[512,512]{1,0:T(8,128)(2,1)S(1)} %copy-done.1) | non-fusion elementwise | flops 262144 | bytes 1572864 | tf_op jit(solution)/shard_map/convert_element_type | solution.py:668
  90.0 0.0 copy-done
  90.0 0.0 copy-start.2
  90.0 1.1 %convert_element_type.15 = f32[512,512]{1,0:T(8,128)} convert(bf16[512,512]{1,0:T(8,128)(2,1)S(1)} %copy-done) | non-fusion elementwise | flops 262144 | bytes 1572864 | tf_op jit(solution)/shard_map/convert_element_type | solution.py:670
  91.1 0.0 copy-done.3
  91.1 0.8 copy.31
  91.9 0.0 copy-done.2
  91.9 0.8 copy.32
  (3 shorter events, 0.1 us)
Async XLA Ops:
  87.5 1.4 %copy-start.1 = (bf16[512,512]{1,0:T(8,128)(2,1)S(1)}, bf16[512,512]{1,0:T(8,128)(2,1)}, u32[]{:S(2)}) copy-start(bf16[512,512]{1,0:T(8,128)(2,1)} %get-tuple-element.28) | copy-start | bytes 1572868
  87.6 2.4 %copy-start = (bf16[512,512]{1,0:T(8,128)(2,1)S(1)}, bf16[512,512]{1,0:T(8,128)(2,1)}, u32[]{:S(2)}) copy-start(bf16[512,512]{1,0:T(8,128)(2,1)} %get-tuple-element.29) | copy-start | bytes 1572868
  88.9 2.2 %copy-start.3 = (bf16[512,512]{1,0:T(8,128)(2,1)S(1)}, bf16[512,512]{1,0:T(8,128)(2,1)}, u32[]{:S(2)}) copy-start(bf16[512,512]{1,0:T(8,128)(2,1)} %get-tuple-element.61) | copy-start | bytes 1572868
  90.0 1.9 %copy-start.2 = (bf16[512,512]{1,0:T(8,128)(2,1)S(1)}, bf16[512,512]{1,0:T(8,128)(2,1)}, u32[]{:S(2)}) copy-start(bf16[512,512]{1,0:T(8,128)(2,1)} %get-tuple-element.62) | copy-start | bytes 1572868

commit v2 on v1

v2 whole, which is shorter than its diff:
```python
import jax
import jax.numpy as jnp
from jax import lax
from jax.experimental import pallas as pl
from jax.experimental.pallas import tpu as pltpu
from jax.sharding import PartitionSpec as P

HD = 128
NORM_EPSILON = 1e-05
MASKED_SCORE = -1e30
LOG2E = 1.4426950408889634
F32 = jnp.float32
BF16 = jnp.bfloat16
MESH = pl.DeviceIdType.MESH


def nn(a, b):
    return lax.dot_general(a, b, (((1,), (0,)), ((), ())), preferred_element_type=F32)


def nt(a, b):
    return lax.dot_general(a, b, (((1,), (1,)), ((), ())), preferred_element_type=F32)


def tn(a, b):
    return lax.dot_general(a, b, (((0,), (0,)), ((), ())), preferred_element_type=F32)


def torus_sizes(chips):
    side = 1
    for k in range(1, chips + 1):
        if chips % (k * k) == 0 and chips // (k * k) >= k:
            side = k
    return side, side, chips // (side * side)


class Semaphores:
    def __init__(self, send_sem, recv_sem):
        self.count = 0
        self.send, self.recv = send_sem, recv_sem

    def take(self, n=1):
        first = self.count
        self.count += n
        return first


def piece_rows(rows, groups):
    sizes = [rows]
    for n, split in groups:
        sizes.append(sizes[-1] // n if split else sizes[-1])
    return sizes


def reduction_scratch(rows, cols, groups):
    sizes = piece_rows(rows, groups)
    specs = [pltpu.VMEM((n - 1, sizes[i + 1], cols), BF16) for i, (n, _) in enumerate(groups)]
    specs += [pltpu.VMEM((sizes[i + 1], cols), BF16) for i in range(len(groups) - 1)]
    return specs


class Reduction:
    def __init__(self, rows, groups, sems, grad, scratch, out):
        self.groups, self.sems, self.out = groups, sems, out
        count = len(groups)
        self.size = piece_rows(rows, [(n, split) for n, _, _, split in groups])
        self.recv = scratch[:count]
        self.held = [grad, *scratch[count:]]
        self.off = [0]
        for i, (n, place, _, split) in enumerate(groups):
            step = self.size[i + 1]
            self.off.append(pl.multiple_of(self.off[i] + place * step, step) if split else self.off[i])
        self.first = [sems.take(n - 1) for n, _, _, _ in groups]
        self.gathers = [i for i in reversed(range(count)) if groups[i][3]]
        self.gather_first = {i: sems.take(groups[i][0] - 1) for i in self.gathers}
        self.last = count + len(self.gathers)

    def copy(self, i, j, first, src, dst):
        n, place, peer, _ = self.groups[i]
        slot = first + j - 1
        return pltpu.make_async_remote_copy(
            src_ref=src,
            dst_ref=dst,
            send_sem=self.sems.send.at[slot],
            recv_sem=self.sems.recv.at[slot],
            device_id=peer(lax.rem(place + j, n)),
            device_id_type=MESH,
        )

    def scatter(self, i):
        n, place, _, split = self.groups[i]
        size = self.size[i + 1]
        copies = []
        for j in range(1, n):
            src = self.held[i]
            if split:
                src = src.at[pl.ds(pl.multiple_of(lax.rem(place + j, n) * size, size), size)]
            copies.append(self.copy(i, j, self.first[i], src, self.recv[i].at[j - 1]))
        return copies

    def gather(self, i, back):
        n, place, _, _ = self.groups[i]
        size = self.size[i + 1]
        copies = []
        for j in range(1, n):
            owner = lax.rem(place + n - j, n) if back else place
            piece = self.out.at[pl.ds(pl.multiple_of(self.off[i] + owner * size, size), size)]
            copies.append(self.copy(i, j, self.gather_first[i], piece, piece))
        return copies

    def total(self, i):
        n, place, _, split = self.groups[i]
        size = self.size[i + 1]
        for c in self.scatter(i):
            c.wait_recv()
        rows = pl.ds(pl.multiple_of(place * size, size), size) if split else slice(None)
        sum_ = self.held[i][rows, :].astype(F32)
        for j in range(n - 1):
            sum_ = sum_ + self.recv[i][j].astype(F32)
        return sum_.astype(BF16)

    def step(self, number):
        count = len(self.groups)
        if number == 0:
            copies = self.scatter(0)
        elif number < count:
            self.held[number][...] = self.total(number - 1)
            copies = self.scatter(number)
        else:
            done = number - count
            if done == 0:
                self.out[pl.ds(self.off[count], self.size[count]), :] = self.total(count - 1)
            else:
                for c in self.gather(self.gathers[done - 1], True):
                    c.wait_recv()
            copies = self.gather(self.gathers[done], False) if done < len(self.gathers) else []
        for c in copies:
            c.start()

    def drain(self):
        for i in range(len(self.groups)):
            for c in self.scatter(i):
                c.wait_send()
        for i in self.gathers:
            for c in self.gather(i, False):
                c.wait_send()


def blk(start, size, align=None):
    return pl.ds(pl.multiple_of(start, align or size), size)


LOOP = {3: ("d0:0", "a1"), 5: ("b1",), 6: ("a2", "c1")}
TAIL = (
    "head1", "d1:0", "sm0", "b2", "d0:1", "c2", "a3", "sm1", "dx_send", "b3", "d0:2", "d1:1", "c3", "dx_keep", "a4", "b4",
    "dx_end", "d1:2", "sm2", "d0:3", "a5", "c4", "b5", "d1:3", "sm3", "d0:4", "c5", "d0:5", "d1:4", "sm4",
    "a6", "b6", "c6", "d0:6",
)


def make_kernel(sizes, length, width, hidden_units):
    nx, ny, nz = sizes
    half = length // 2
    qb = 256
    fh = hidden_units // 2
    heads = 2
    hw = heads * HD
    kcat = 3 * HD
    blocks = length // qb
    score_c = HD ** (-0.5) * LOG2E

    def split_z(rows):
        return rows % (nx * ny * nz) == 0 and (rows // (nx * ny * nz)) % 16 == 0

    grads = dict(a=(fh, width), b=(width, fh), c=(hw, width), d0=(width, kcat), d1=(width, kcat))
    plane = ("d1",)

    def group_sizes(name):
        z = (nz, split_z(grads[name][0]))
        return [(nx * ny, True), z] if name in plane else [(nx, True), (ny, True), z]

    scratch = dict(
        x=pltpu.VMEM((length, width), BF16),
        wqkv=pltpu.VMEM((3, width, hw), BF16),
        wout=pltpu.VMEM((hw, width), BF16),
        win=pltpu.VMEM((width, fh), BF16),
        wdown=pltpu.VMEM((fh, width), BF16),
        dout=pltpu.VMEM((half, width), BF16),
        output=pltpu.VMEM((half, width), BF16),
        xt=pltpu.VMEM((width, length), BF16),
        q=pltpu.VMEM((heads, length, HD), BF16),
        k=pltpu.VMEM((heads, length, HD), BF16),
        v=pltpu.VMEM((heads, length, HD), BF16),
        kt=pltpu.VMEM((heads, HD, length), BF16),
        vt=pltpu.VMEM((heads, HD, length), BF16),
        segf=pltpu.VMEM((1, length), F32),
        kb=pltpu.VMEM((length, qb), F32),
        weights=pltpu.VMEM((heads, blocks, length, qb), BF16),
        inv=pltpu.VMEM((heads, length, HD), F32),
        mix=pltpu.VMEM((heads, length, HD), BF16),
        mo=pltpu.VMEM((heads, half, HD), BF16),
        wout_o=pltpu.VMEM((hw, width), BF16),
        win_o=pltpu.VMEM((width, fh), BF16),
        wdown_o=pltpu.VMEM((fh, width), BF16),
        bin_o=pltpu.VMEM((1, fh), F32),
        hid=pltpu.VMEM((half, width), BF16),
        act=pltpu.VMEM((2, half, fh), BF16),
        gp=pltpu.VMEM((2, qb, fh), F32),
        ddown=pltpu.VMEM((half, width), BF16),
        dup=pltpu.VMEM((2, half, fh), BF16),
        dattn=pltpu.VMEM((half, width), BF16),
        dpre=pltpu.VMEM((half, width), F32),
        dmix=pltpu.VMEM((heads, length, HD), BF16),
        dmo=pltpu.VMEM((heads, half, HD), BF16),
        dkacc=pltpu.VMEM((heads, length, HD), F32),
        dvacc=pltpu.VMEM((heads, length, HD), F32),
        dcat=pltpu.VMEM((heads, length, kcat), BF16),
        dxs=pltpu.VMEM((half, width), BF16),
        dxr=pltpu.VMEM((half, width), BF16),
        din=pltpu.VMEM((half, width), BF16),
        sm=pltpu.VMEM((16, width), F32),
        smt=pltpu.VMEM((16, width), F32),
        sm0=pltpu.VMEM((16, width), F32),
        sm1=pltpu.VMEM((16, width), F32),
        sm2=pltpu.VMEM((16, width), F32),
        sm3=pltpu.VMEM((16, width), F32),
        smr1=pltpu.VMEM((nx - 1, 16, width), F32),
        smr2=pltpu.VMEM((ny - 1, 16, width), F32),
        smr3=pltpu.VMEM((nz - 1, 16, width), F32),
    )
    n_sems = 4 + 2 * heads + 3 + 1 + 1 + (nx + ny + nz - 3)
    n_local = 2 * blocks + 16
    for name, (rows, cols) in grads.items():
        scratch["g_" + name] = pltpu.VMEM((rows, cols), BF16)
        scratch["o_" + name] = pltpu.VMEM((rows, cols), BF16)
        if name in "abc":
            scratch["gs_" + name] = pltpu.VMEM((rows, cols), BF16)
            scratch["gr_" + name] = pltpu.VMEM((rows, cols), BF16)
        for i, spec in enumerate(reduction_scratch(rows, cols, group_sizes(name))):
            scratch[f"red_{name}_{i}"] = spec
        n_sems += sum((n - 1) * (2 if split else 1) for n, split in group_sizes(name))
    names = list(scratch)

    def kernel(x_h, wqkv_h, bqv, wout_h, bout, n1g, n1s, win_h, bin_, wdown_h, bdown, n2g, n2s, seg, dout_h, *rest):
        out_h, din_h, ga_h, gb_h, gc_h, gd0_h, gd1_h, small_o = rest[:8]
        refs = dict(zip(names, rest[8 : 8 + len(names)]))
        send_sem, recv_sem, local_sem = rest[8 + len(names) :]
        s = type("Scratch", (), refs)
        sems = Semaphores(send_sem, recv_sem)

        dp = lax.axis_index("dp")
        t = lax.axis_index("tensor")
        other = 1 - t
        xi = lax.rem(dp, nx)
        yi = lax.rem(lax.div(dp, nx), ny)
        zi = lax.div(dp, nx * ny)
        qi = lax.rem(dp, nx * ny)
        m1 = xi + t * (yi - xi)
        m2 = yi + t * (xi - yi)
        stride1 = 1 + t * (nx - 1)
        stride2 = nx + t * (1 - nx)
        peer1 = lambda c: (dp + (c - m1) * stride1, t)
        peer2 = lambda c: (dp + (c - m2) * stride2, t)
        peer3 = lambda c: (dp + (c - zi) * (nx * ny), t)
        peer_q = lambda c: (dp + (c - qi), t)

        barrier = pltpu.get_barrier_semaphore()

        def greet(device):
            pl.semaphore_signal(barrier, inc=1, device_id=device, device_id_type=MESH)

        greet((dp, other))
        for n, m, peer in ((nx * ny, qi, peer_q), (nz, zi, peer3)):
            for j in range(1, n):
                greet(peer(lax.rem(m + j, n)))

        local = Semaphores(None, local_sem)

        def load(src, dst):
            c = pltpu.make_async_copy(src, dst, local_sem.at[local.take()])
            c.start()
            return c

        x_in = [None] * blocks
        x_in[0] = load(x_h.at[pl.ds(0, qb)], s.x.at[pl.ds(0, qb)])
        wqkv_in = load(wqkv_h, s.wqkv)
        for i in range(1, blocks):
            x_in[i] = load(x_h.at[pl.ds(i * qb, qb)], s.x.at[pl.ds(i * qb, qb)])
        weights_in = [load(wout_h, s.wout), load(win_h, s.win), load(wdown_h, s.wdown), load(dout_h, s.dout)]
        stores = []

        def store(src, dst):
            stores.append(load(src, dst))

        def across(src, dst, slot=None):
            slot = sems.take() if slot is None else slot
            return pltpu.make_async_remote_copy(
                src_ref=src, dst_ref=dst, send_sem=send_sem.at[slot], recv_sem=recv_sem.at[slot],
                device_id=(dp, other), device_id_type=MESH,
            )

        my0 = pl.multiple_of(t * half, half)
        ot0 = pl.multiple_of(other * half, half)
        all_copies = []

        def launch(*copies):
            for c in copies:
                c.start()
                all_copies.append(c)

        red = {}
        for name, (rows, cols) in grads.items():
            z = (nz, zi, peer3, split_z(rows))
            if name in plane:
                groups = [(nx * ny, qi, peer_q, True), z]
            else:
                groups = [(nx, m1, peer1, True), (ny, m2, peer2, True), z]
            bufs = [refs[f"red_{name}_{i}"] for i in range(2 * len(groups) - 1)]
            red[name] = Reduction(rows, groups, sems, refs["g_" + name], bufs, refs["o_" + name])
        hbm_out = dict(a=ga_h, b=gb_h, c=gc_h, d0=gd0_h, d1=gd1_h)
        at = dict.fromkeys(grads, 0)

        def advance(name, number):
            if number > red[name].last:
                return
            assert at[name] == number
            at[name] += 1
            red[name].step(number)
            if number == red[name].last:
                store(refs["o_" + name], hbm_out[name])

        segf = seg[...].astype(F32)
        s.segf[...] = segf
        for b in range(length // 128):
            rows = jnp.broadcast_to(s.segf[:, b * 128 : (b + 1) * 128], (128, 128)).T
            for c in range(qb // 128):
                s.kb[b * 128 : (b + 1) * 128, c * 128 : (c + 1) * 128] = rows

        def project(rows):
            xb = s.x[rows, :]
            s.xt[:, rows] = xb.T
            qv = nn(xb, s.wqkv[0]) + bqv[0:1, :]
            kv = nn(xb, s.wqkv[1])
            vv = nn(xb, s.wqkv[2]) + bqv[1:2, :]
            ql, kl, vl = qv.astype(BF16), kv.astype(BF16), vv.astype(BF16)
            for h in range(heads):
                cols = slice(h * HD, (h + 1) * HD)
                s.q[h, rows, :] = ql[:, cols]
                s.k[h, rows, :] = kl[:, cols]
                s.v[h, rows, :] = vl[:, cols]
                s.kt[h, :, rows] = kl[:, cols].T
                s.vt[h, :, rows] = vl[:, cols].T

        x_in[0].wait()
        wqkv_in.wait()
        project(pl.ds(0, qb))
        for c in x_in[1:]:
            c.wait()

        def project_rest(i, _):
            project(blk(i * qb, qb))
            return 0

        lax.fori_loop(1, blocks, project_rest, 0)
        pl.semaphore_wait(barrier, 1 + (nx * ny - 1) + (nz - 1))
        weights = [across(wout_h, s.wout_o), across(win_h, s.win_o), across(wdown_h, s.wdown_o), across(bin_, s.bin_o)]
        launch(*weights)

        def attend(i, _):
            h = lax.rem(i, heads)
            qi = lax.rem(other * (blocks // 2) + lax.div(i, heads), blocks)
            rows = blk(qi * qb, qb)
            products = nt(s.k[h], s.q[h, rows, :]) * score_c
            scores = jnp.where(s.kb[...] == s.segf[:, rows], products, MASKED_SCORE)
            top = jnp.max(scores, 0, keepdims=True)
            weights_t = jnp.exp2(scores - top)
            inverse = 1.0 / jnp.sum(weights_t, 0, keepdims=True)
            low = weights_t.astype(BF16)
            s.weights[h, qi] = low
            mixed = nn(s.vt[h], low) * inverse
            s.mix[h, rows, :] = mixed.T.astype(BF16)
            s.inv[h, rows, :] = jnp.broadcast_to(inverse, (HD, qb)).T
            return 0

        n_att = heads * blocks
        lax.fori_loop(0, n_att // 2, attend, 0)
        mix_out = [across(s.mix.at[h, pl.ds(ot0, half)], s.mo.at[h]) for h in range(heads)]
        launch(*mix_out)
        lax.fori_loop(n_att // 2, n_att, attend, 0)
        for c in weights_in:
            c.wait()
        for c in weights + mix_out:
            c.wait_recv()

        s.sm[...] = jnp.zeros_like(s.sm)

        def add_small(row, value):
            s.sm[row : row + 1, :] += value

        def row_sum(value):
            return jnp.sum(value, 0, keepdims=True)

        def norm(v):
            average = jnp.mean(v, -1, keepdims=True)
            centred = v - average
            rs = lax.rsqrt(jnp.mean(centred * centred, -1, keepdims=True) + NORM_EPSILON)
            return centred * rs, rs

        def norm_back(e, n, rs):
            return (e - jnp.mean(e, -1, keepdims=True) - n * jnp.mean(e * n, -1, keepdims=True)) * rs

        halves = ((s.win, bin_, s.wdown, s.wout), (s.win_o, s.bin_o, s.wdown_o, s.wout_o))

        def middle(r, _):
            here = blk(r * qb, qb)
            whole = pl.ds(pl.multiple_of(my0 + r * qb, qb), qb)
            mine = jnp.concatenate([s.mix[h, whole, :] for h in range(heads)], 1)
            theirs = jnp.concatenate([s.mo[h, here, :] for h in range(heads)], 1)
            pre1 = s.x[whole, :].astype(F32) + (nn(mine, s.wout[...]) + nn(theirs, s.wout_o[...]) + bout[...])
            n1, rs1 = norm(pre1)
            hidden = n1 * n1g[...] + n1s[...]
            low = hidden.astype(BF16)
            s.hid[here, :] = low
            for f, (w_in, b_in, _, _) in enumerate(halves):
                up = nn(low, w_in[...]) + b_in[...]
                cdf = 0.5 * (1.0 + lax.erf(up * (0.5**0.5)))
                s.act[f, here, :] = (up * cdf).astype(BF16)
                s.gp[f] = cdf + up * (jnp.exp2(up * up * (-0.5 * LOG2E)) * 0.3989422804014327)
            down = nn(s.act[0, here, :], s.wdown[...]) + nn(s.act[1, here, :], s.wdown_o[...]) + bdown[...]
            n2, rs2 = norm(hidden + down)
            row_mask = (s.kb[whole, 0:1] != 0.0).astype(F32)
            s.output[here, :] = ((n2 * n2g[...] + n2s[...]) * row_mask).astype(BF16)
            cot = s.dout[here, :].astype(F32) * row_mask
            add_small(0, row_sum(cot))
            add_small(1, row_sum(cot * n2))
            d_resid = norm_back(cot * n2g[...], n2, rs2)
            d_down = d_resid.astype(BF16)
            s.ddown[here, :] = d_down
            add_small(2, row_sum(d_down.astype(F32)))
            d_hidden = d_resid
            for f, (w_in, _, w_down, _) in enumerate(halves):
                d_up = (nt(d_down, w_down[...]) * s.gp[f]).astype(BF16)
                s.dup[f, here, :] = d_up
                add_small(3 + f, row_sum(d_up.astype(F32)))
                d_hidden = d_hidden + nt(d_up, w_in[...])
            add_small(5, row_sum(d_hidden))
            add_small(6, row_sum(d_hidden * n1))
            d_pre = norm_back(d_hidden * n1g[...], n1, rs1)
            s.dpre[here, :] = d_pre
            d_attn = d_pre.astype(BF16)
            s.dattn[here, :] = d_attn
            add_small(7, row_sum(d_attn.astype(F32)))
            dm = nt(d_attn, s.wout[...]).astype(BF16)
            do = nt(d_attn, s.wout_o[...]).astype(BF16)
            for h in range(heads):
                s.dmix[h, whole, :] = dm[:, h * HD : (h + 1) * HD]
                s.dmo[h, here, :] = do[:, h * HD : (h + 1) * HD]
            return 0

        lax.fori_loop(0, half // qb, middle, 0)
        dmix_slots = [sems.take() for _ in range(heads)]
        launch(*[across(s.dmo.at[h], s.dmix.at[h, pl.ds(my0, half)], dmix_slots[h]) for h in range(heads)])
        store(s.output, out_h)

        def grad_block(dst, lhs, rhs):
            def body(i, _):
                cols = blk(i * qb, qb)
                dst[cols, :] = tn(lhs[:, cols], rhs[...]).astype(BF16)
                return 0

            lax.fori_loop(0, lhs.shape[1] // qb, body, 0)

        part = {name: across(refs["gs_" + name], refs["gr_" + name]) for name in "abc"}

        def join(name):
            part[name].wait_recv()
            mine, theirs = refs["g_" + name], refs["gr_" + name]
            mine[...] = (mine[...].astype(F32) + theirs[...].astype(F32)).astype(BF16)
            advance(name, 0)

        grad_block(s.gs_a, s.act.at[1], s.ddown)
        launch(part["a"])
        grad_block(s.g_a, s.act.at[0], s.ddown)
        grad_block(s.gs_b, s.hid, s.dup.at[1])
        launch(part["b"])
        join("a")
        grad_block(s.g_b, s.hid, s.dup.at[0])
        theirs = jnp.concatenate([s.mo[h] for h in range(heads)], 1)
        s.gs_c[...] = tn(theirs, s.dattn[...]).astype(BF16)
        launch(part["c"])
        join("b")
        mine = jnp.concatenate([s.mix[h, pl.ds(my0, half), :] for h in range(heads)], 1)
        s.g_c[...] = tn(mine, s.dattn[...]).astype(BF16)
        join("c")

        s.dkacc[...] = jnp.zeros_like(s.dkacc)
        s.dvacc[...] = jnp.zeros_like(s.dvacc)
        for h in range(heads):
            across(s.dmo.at[h], s.dmix.at[h, pl.ds(ot0, half)], dmix_slots[h]).wait_recv()

        def finish_head(h):
            dk = (s.dkacc[h] * (HD ** (-0.5))).astype(BF16)
            dv = s.dvacc[h].astype(BF16)
            s.dcat[h, :, HD : 2 * HD] = dk
            s.dcat[h, :, 2 * HD :] = dv
            s.sm[8:9, h * HD : (h + 1) * HD] = row_sum(s.dcat[h, :, 0:HD].astype(F32))
            s.sm[8:9, hw + h * HD : hw + (h + 1) * HD] = row_sum(dv.astype(F32))
            dst = s.g_d0 if h == 0 else s.g_d1

            def body(i, _):
                rows = blk(i * 128, 128)
                dst[rows, :] = nn(s.xt[rows, :], s.dcat[h]).astype(BF16)
                return 0

            lax.fori_loop(0, width // 128, body, 0)

        def advance_all(tokens):
            for token in tokens:
                name, number = token.split(":") if ":" in token else (token[0], token[1:])
                advance(name, int(number))

        def attend_back(i, _):
            h = lax.div(i, blocks)
            qi = lax.rem(t * (blocks // 2) + lax.rem(i, blocks), blocks)
            rows = blk(qi * qb, qb)
            d_mixed = s.dmix[h, rows, :].astype(F32) * s.inv[h, rows, :]
            delta = row_sum((d_mixed * s.mix[h, rows, :].astype(F32)).T)
            d_low = d_mixed.astype(BF16)
            weights_t = s.weights[h, qi]
            s.dvacc[h] += nn(weights_t, d_low)
            d_scores = (weights_t.astype(F32) * (nt(s.v[h], d_low) - delta)).astype(BF16)
            s.dkacc[h] += nn(d_scores, s.q[h, rows, :])
            dqt = nn(s.kt[h], d_scores) * (HD ** (-0.5))
            s.dcat[h, rows, 0:HD] = dqt.T.astype(BF16)
            for number, tokens in LOOP.items():

                @pl.when(i == number)
                def _():
                    if number == blocks - 1:
                        finish_head(0)
                    advance_all(tokens)

            return 0

        lax.fori_loop(0, n_att, attend_back, 0)

        def project_back(i):
            rows = blk(lax.rem(other * (blocks // 2) + i, blocks) * qb, qb)
            wide = jnp.concatenate([s.dcat[h, rows, :] for h in range(heads)], 1)
            wcat = jnp.concatenate(
                [s.wqkv[c][:, h * HD : (h + 1) * HD] for h in range(heads) for c in range(3)], 1
            )
            return nt(wide, wcat)

        def send_rows(i, _):
            s.dxs[blk(i * qb, qb), :] = project_back(i).astype(BF16)
            return 0

        def keep_rows(i, _):
            s.dpre[blk((i - blocks // 2) * qb, qb), :] += project_back(i)
            return 0

        dx_out = across(s.dxs, s.dxr)
        small_t = across(s.sm, s.smt)
        small_groups = ((nx, m1, peer1), (ny, m2, peer2), (nz, zi, peer3))
        small_bufs = ((s.sm0, s.smr1, s.sm1), (s.sm1, s.smr2, s.sm2), (s.sm2, s.smr3, s.sm3))
        small_first = [sems.take(n - 1) for n, _, _ in small_groups]
        assert sems.count == n_sems

        def small_copies(i):
            n, m, peer = small_groups[i]
            src, dst, _ = small_bufs[i]
            return [
                pltpu.make_async_remote_copy(
                    src_ref=src, dst_ref=dst.at[j - 1], send_sem=send_sem.at[small_first[i] + j - 1],
                    recv_sem=recv_sem.at[small_first[i] + j - 1], device_id=peer(lax.rem(m + j, n)), device_id_type=MESH,
                )
                for j in range(1, n)
            ]

        def small_step(number):
            if number == 0:
                launch(small_t)
                return
            if number == 1:
                small_t.wait_recv()
                s.sm0[...] = s.sm[...] + s.smt[...]
                s.sm0[3:4, :] = s.sm[3:4, :] + s.smt[4:5, :]
                s.sm0[8:9, :] = s.sm[8:9, :]
            else:
                src, got, dst = small_bufs[number - 2]
                for c in small_copies(number - 2):
                    c.wait_recv()
                total = src[...]
                for j in range(small_groups[number - 2][0] - 1):
                    total = total + got[j]
                dst[...] = total
            if number <= 3:
                for c in small_copies(number - 1):
                    c.start()
            else:
                small_o[...] = s.sm3[...]

        for token in TAIL:
            if token == "head1":
                finish_head(1)
            elif token == "dx_send":
                lax.fori_loop(0, blocks // 2, send_rows, 0)
                launch(dx_out)
            elif token == "dx_keep":
                lax.fori_loop(blocks // 2, blocks, keep_rows, 0)
            elif token == "dx_end":
                dx_out.wait_recv()
                s.din[...] = (s.dpre[...] + s.dxr[...].astype(F32)).astype(BF16)
                store(s.din, din_h)
            elif token.startswith("sm"):
                small_step(int(token[2:]))
            else:
                advance_all([token])
        for name in grads:
            while at[name] <= red[name].last:
                advance(name, at[name])
        for c in all_copies:
            c.wait_send()
        for i in range(3):
            for c in small_copies(i):
                c.wait_send()
        for r in red.values():
            r.drain()
        for c in stores:
            c.wait()

    return kernel, list(scratch.values()), n_sems, n_local, grads


def finish_kernel(grads, half, width, hw):
    def kernel(out_i, din_i, ga, gb, gc, gd0, gd1, small, out_o, din_o, gqkv_o, gout_o, gin_o, gdown_o, bqv_o, *rest):
        rows_o, (v_out, v_din, va, vb, vc, vd0, vd1, fa, fb, fc, fqkv, sems) = rest[:7], rest[7:]
        loads = [
            pltpu.make_async_copy(src, dst, sems.at[i])
            for i, (src, dst) in enumerate(
                ((ga, va), (gb, vb), (gd0, vd0), (gd1, vd1), (gc, vc), (out_i, v_out), (din_i, v_din))
            )
        ]
        stores = [
            pltpu.make_async_copy(src, dst, sems.at[8 + i])
            for i, (src, dst) in enumerate(
                ((fa, gdown_o), (fb, gin_o), (fqkv, gqkv_o), (fc, gout_o), (v_out, out_o), (v_din, din_o))
            )
        ]
        for c in loads:
            c.start()
        for row, ref in zip((7, 6, 5, 3, 2, 1, 0), rows_o):
            ref[...] = small[row : row + 1, :]
        for i in range(2):
            bqv_o[i : i + 1, :] = small[8:9, i * hw : (i + 1) * hw]
        loads[0].wait()
        fa[...] = va[...].astype(F32)
        stores[0].start()
        loads[1].wait()
        fb[...] = vb[...].astype(F32)
        stores[1].start()
        for h, (load, src) in enumerate(((loads[2], vd0), (loads[3], vd1))):
            load.wait()
            for c in range(3):
                fqkv[c, :, h * HD : (h + 1) * HD] = src[:, c * HD : (c + 1) * HD].astype(F32)
        stores[2].start()
        loads[4].wait()
        fc[...] = vc[...].astype(F32)
        stores[3].start()
        loads[5].wait()
        stores[4].start()
        loads[6].wait()
        stores[5].start()
        for c in stores:
            c.wait()

    fh = grads["a"][0]
    shapes = [
        jax.ShapeDtypeStruct((half, width), BF16),
        jax.ShapeDtypeStruct((half, width), BF16),
        jax.ShapeDtypeStruct((3, width, hw), F32),
        jax.ShapeDtypeStruct((hw, width), F32),
        jax.ShapeDtypeStruct((width, fh), F32),
        jax.ShapeDtypeStruct((fh, width), F32),
        jax.ShapeDtypeStruct((2, hw), F32),
        *[jax.ShapeDtypeStruct((1, width), F32)] * 7,
    ]
    any_ = pl.BlockSpec(memory_space=pl.ANY)
    vmem = pl.BlockSpec(memory_space=pltpu.VMEM)
    vm = pltpu.VMEM
    return pl.pallas_call(
        kernel,
        out_shape=shapes,
        in_specs=[any_] * 7 + [vmem],
        out_specs=[any_] * 6 + [vmem] * 8,
        scratch_shapes=[
            vm((half, width), BF16),
            vm((half, width), BF16),
            *[vm(grads[n], BF16) for n in grads],
            *[vm(grads[n], F32) for n in "abc"],
            vm((3, width, hw), F32),
            pltpu.SemaphoreType.DMA((16,)),
        ],
        compiler_params=pltpu.CompilerParams(vmem_limit_bytes=63 * 1024 * 1024),
    )


def solution(mesh):
    chips = mesh.shape["dp"]
    sizes = torus_sizes(chips)

    def on_device(
        inputs, w_qkv, b_qv, w_out, b_out, norm1_gain, norm1_shift, w_in, b_in, w_down, b_down, norm2_gain, norm2_shift,
        segment_ids, d_out,
    ):
        length, width = inputs.shape
        fh = w_in.shape[1]
        hw = w_out.shape[0]
        half = length // 2
        kernel, scratch, n_sems, n_local, grads = make_kernel(sizes, length, width, 2 * fh)
        row = lambda v: v.reshape(1, -1)
        vmem = pl.BlockSpec(memory_space=pltpu.VMEM)
        any_ = pl.BlockSpec(memory_space=pl.ANY)
        shapes = [
            jax.ShapeDtypeStruct((half, width), BF16),
            jax.ShapeDtypeStruct((half, width), BF16),
            *[jax.ShapeDtypeStruct(shape, BF16) for shape in grads.values()],
            jax.ShapeDtypeStruct((16, width), F32),
        ]
        dma = pltpu.SemaphoreType.DMA
        partial_results = pl.pallas_call(
            kernel,
            out_shape=shapes,
            in_specs=[any_, any_, vmem, any_, vmem, vmem, vmem, any_, vmem, any_, vmem, vmem, vmem, vmem, any_],
            out_specs=[any_] * 7 + [vmem],
            scratch_shapes=[*scratch, dma((n_sems,)), dma((n_sems,)), dma((n_local,))],
            compiler_params=pltpu.CompilerParams(
                collective_id=0, has_side_effects=True, vmem_limit_bytes=60 * 1024 * 1024
            ),
        )(
            inputs, w_qkv, b_qv, w_out, row(b_out), row(norm1_gain), row(norm1_shift), w_in, row(b_in), w_down,
            row(b_down), row(norm2_gain), row(norm2_shift), segment_ids, d_out,
        )
        output, d_inputs, g_qkv, g_out, g_in, g_down, g_bqv, *rows = finish_kernel(grads, half, width, hw)(*partial_results)
        g_bout, g_n1g, g_n1s, g_bin, g_bdown, g_n2g, g_n2s = [v.reshape(-1) for v in rows]
        return (
            output, d_inputs, g_qkv, g_bqv, g_out, g_bout, g_n1g, g_n1s, g_in, g_bin, g_down, g_bdown, g_n2g, g_n2s,
        )

    placed = (
        P("dp", None),
        P(None, None, "tensor"),
        P(None, "tensor"),
        P("tensor", None),
        P(),
        P(),
        P(),
        P(None, "tensor"),
        P("tensor"),
        P("tensor", None),
        P(),
        P(),
        P(),
        P("dp", None),
        P(("dp", "tensor"), None),
    )
    return jax.shard_map(
        on_device,
        mesh=mesh,
        in_specs=placed,
        out_specs=(
            P(("dp", "tensor"), None),
            P(("dp", "tensor"), None),
            P(None, None, "tensor"),
            P(None, "tensor"),
            P("tensor", None),
            P(),
            P(),
            P(),
            P(None, "tensor"),
            P("tensor"),
            P("tensor", None),
            P(),
            P(),
            P(),
        ),
        check_vma=False,
    )
```

time: 92.9 us -> 80.3 us (0.86)
  other arithmetic: 5.37 us -> 0 us
  local copies, waits for them, and re-layouts: 5.04 us -> 0 us
  Pallas kernels: 81.6 us -> 79.4 us
    convert_element_type x4 -> x0, other arithmetic: 5.28 us -> none  [the longest x1 1.8 us: on_device(): gc.astype(F32)]
    slice x2 -> x0, local copies, waits for them, and re-layouts: 2.84 us -> none  [the longest x1 1.59 us: on_device(): small[0]]
    pallas_call x1 -> x2, Pallas kernels: 81.6 us -> 79.4 us  [the longest x1 74.4 us: on_device(): pl.pallas_call(kernel, out_shape=shapes, in_specs=[any_, any_, vmem, any_...]
    unnamed x10 -> x0, local copies, waits for them, and re-layouts: 1.6 us -> none
where the time goes in v2:
time: 80.3 us; the launch traced here: 80.1 us
  Pallas kernels  79.4 us (99%)
    pallas_call x1, Pallas kernels, on_device(): pl.pallas_call(kernel, out_shape=shapes, in_specs=[any_, any_, vmem, any_...  74.4 us
    pallas_call x1, Pallas kernels, on_device(): finish_kernel(grads, half, width, hw)(*partial_results)  4.96 us

profile of v2, /device:TPU:0, one launch (start us, length us, event | category | flops | bytes accessed | tf_op | source)
XLA Modules:
  0.0 80.1 jit_solution(9456067286828887062)
XLA Ops:
  0.7 74.4 %shard_map.254 = (bf16[512,512]{1,0:T(8,128)(2,1)}, bf16[512,512]{1,0:T(8,128)(2,1)}, bf16[512,512]{1,0:T(8,128)(2,1)}, bf16[512,512]{1,0:T(8,128)(2,1)}, bf16[2...) custom-call(bf16[1024,512]{1,0:T(8,128)(2,1)} %x_h.1, ...), custom_call_target="tpu_custom_call" | custom-call | tf_op jit(solution)/shard_map/pallas_call | solution.py:732
  75.1 5.0 %shard_map.255 = (bf16[512,512]{1,0:T(8,128)(2,1)}, bf16[512,512]{1,0:T(8,128)(2,1)}, f32[3,512,256]{2,1,0:T(8,128)}, f32[256,512]{1,0:T(8,128)}, f32[512,512]{1...) custom-call(bf16[512,512]{1,0:T(8,128)(2,1)} %get-tuple-element.36.o, ...), custom_call_target="tpu_custom_call" | custom-call | tf_op jit(solution)/shard_map/pallas_call | solution.py:745

commit v3 on v2

--- a/solution.py
+++ b/solution.py
@@ -70,14 +70,13 @@
         for i, (n, place, _, split) in enumerate(groups):
             step = self.size[i + 1]
             self.off.append(pl.multiple_of(self.off[i] + place * step, step) if split else self.off[i])
-        self.first = [sems.take(n - 1) for n, _, _, _ in groups]
+        self.slot = [sems.take() for _ in groups]
         self.gathers = [i for i in reversed(range(count)) if groups[i][3]]
-        self.gather_first = {i: sems.take(groups[i][0] - 1) for i in self.gathers}
+        self.gather_slot = {i: sems.take() for i in self.gathers}
         self.last = count + len(self.gathers)
 
-    def copy(self, i, j, first, src, dst):
+    def copy(self, i, j, slot, src, dst):
         n, place, peer, _ = self.groups[i]
-        slot = first + j - 1
         return pltpu.make_async_remote_copy(
             src_ref=src,
             dst_ref=dst,
@@ -95,24 +94,22 @@
             src = self.held[i]
             if split:
                 src = src.at[pl.ds(pl.multiple_of(lax.rem(place + j, n) * size, size), size)]
-            copies.append(self.copy(i, j, self.first[i], src, self.recv[i].at[j - 1]))
+            copies.append(self.copy(i, j, self.slot[i], src, self.recv[i].at[j - 1]))
         return copies
 
-    def gather(self, i, back):
+    def gather(self, i):
         n, place, _, _ = self.groups[i]
         size = self.size[i + 1]
-        copies = []
-        for j in range(1, n):
-            owner = lax.rem(place + n - j, n) if back else place
-            piece = self.out.at[pl.ds(pl.multiple_of(self.off[i] + owner * size, size), size)]
-            copies.append(self.copy(i, j, self.gather_first[i], piece, piece))
-        return copies
+        piece = self.out.at[pl.ds(pl.multiple_of(self.off[i] + place * size, size), size)]
+        return [self.copy(i, j, self.gather_slot[i], piece, piece) for j in range(1, n)]
+
+    def all_of(self, i, slot):
+        return self.copy(i, 1, slot, self.recv[i], self.recv[i])
 
     def total(self, i):
         n, place, _, split = self.groups[i]
         size = self.size[i + 1]
-        for c in self.scatter(i):
-            c.wait_recv()
+        self.all_of(i, self.slot[i]).wait_recv()
         rows = pl.ds(pl.multiple_of(place * size, size), size) if split else slice(None)
         sum_ = self.held[i][rows, :].astype(F32)
         for j in range(n - 1):
@@ -131,31 +128,39 @@
             if done == 0:
                 self.out[pl.ds(self.off[count], self.size[count]), :] = self.total(count - 1)
             else:
-                for c in self.gather(self.gathers[done - 1], True):
-                    c.wait_recv()
-            copies = self.gather(self.gathers[done], False) if done < len(self.gathers) else []
+                last = self.gathers[done - 1]
+                self.all_of(last, self.gather_slot[last]).wait_recv()
+            copies = self.gather(self.gathers[done]) if done < len(self.gathers) else []
         for c in copies:
             c.start()
 
     def drain(self):
         for i in range(len(self.groups)):
-            for c in self.scatter(i):
-                c.wait_send()
+            self.all_of(i, self.slot[i]).wait_send()
         for i in self.gathers:
-            for c in self.gather(i, False):
-                c.wait_send()
+            self.all_of(i, self.gather_slot[i]).wait_send()
 
 
 def blk(start, size, align=None):
     return pl.ds(pl.multiple_of(start, align or size), size)
 
 
-LOOP = {3: ("d0:0", "a1"), 5: ("b1",), 6: ("a2", "c1")}
+LOOP = {
+    1: ("a.0:1",),
+    2: ("a.1:1",),
+    3: ("head0", "b.0:1", "a.0:2"),
+    4: ("a.1:2", "b.1:1"),
+    6: ("c.0:1", "c.1:1", "d0.0:1", "b.0:2"),
+    7: ("d0.1:1", "b.1:2"),
+}
 TAIL = (
-    "head1", "d1:0", "sm0", "b2", "d0:1", "c2", "a3", "sm1", "dx_send", "b3", "d0:2", "d1:1", "c3", "dx_keep", "a4", "b4",
-    "dx_end", "d1:2", "sm2", "d0:3", "a5", "c4", "b5", "d1:3", "sm3", "d0:4", "c5", "d0:5", "d1:4", "sm4",
-    "a6", "b6", "c6", "d0:6",
+    "head1", "d0.2:1", "a.0:3", "d0.0:2", "a.1:3", "sm0", "dx_send", "d0.1:2", "c.0:2", "sm1", "dx_keep", "dx_end",
+    "sm2", "c.1:2", "b.0:3", "d1.0:1", "b.1:3", "d1.1:1", "d0.2:2", "a.0:4", "d1.2:1", "sm3", "d0.0:3", "a.1:4",
+    "d0.1:3", "c.0:3", "a.0:5", "c.1:3", "b.0:4", "a.1:5", "d1.0:2", "b.1:4", "c.0:4", "d1.1:2", "sm4", "d0.2:3",
+    "d1.2:2", "a.0:6", "b.0:5", "d0.0:4", "d0.1:4", "c.1:4", "b.1:5", "d1.0:3", "a.1:6", "d1.1:3", "d0.0:5", "d0.2:4",
+    "d0.1:5", "b.0:6", "d1.2:3", "b.1:6", "d0.2:5", "d1.0:4", "d1.1:4", "d0.0:6", "d0.1:6", "d0.2:6", "d1.2:4",
 )
+PARTS = dict(a=2, b=2, c=2, d0=3, d1=3)
 
 
 def make_kernel(sizes, length, width, hidden_units):
@@ -173,7 +178,7 @@
         return rows % (nx * ny * nz) == 0 and (rows // (nx * ny * nz)) % 16 == 0
 
     grads = dict(a=(fh, width), b=(width, fh), c=(hw, width), d0=(width, kcat), d1=(width, kcat))
-    plane = ("d1",)
+    plane = ("c", "d1")
 
     def group_sizes(name):
         z = (nz, split_z(grads[name][0]))
@@ -236,9 +241,10 @@
         if name in "abc":
             scratch["gs_" + name] = pltpu.VMEM((rows, cols), BF16)
             scratch["gr_" + name] = pltpu.VMEM((rows, cols), BF16)
-        for i, spec in enumerate(reduction_scratch(rows, cols, group_sizes(name))):
-            scratch[f"red_{name}_{i}"] = spec
-        n_sems += sum((n - 1) * (2 if split else 1) for n, split in group_sizes(name))
+        for p in range(PARTS[name]):
+            for i, spec in enumerate(reduction_scratch(rows, cols // PARTS[name], group_sizes(name))):
+                scratch[f"red_{name}.{p}_{i}"] = spec
+            n_sems += sum(2 if split else 1 for _, split in group_sizes(name))
     names = list(scratch)
 
     def kernel(x_h, wqkv_h, bqv, wout_h, bout, n1g, n1s, win_h, bin_, wdown_h, bdown, n2g, n2s, seg, dout_h, *rest):
@@ -315,10 +321,13 @@
                 groups = [(nx * ny, qi, peer_q, True), z]
             else:
                 groups = [(nx, m1, peer1, True), (ny, m2, peer2, True), z]
-            bufs = [refs[f"red_{name}_{i}"] for i in range(2 * len(groups) - 1)]
-            red[name] = Reduction(rows, groups, sems, refs["g_" + name], bufs, refs["o_" + name])
+            for p in range(PARTS[name]):
+                bufs = [refs[f"red_{name}.{p}_{i}"] for i in range(2 * len(groups) - 1)]
+                here = pl.ds(p * (cols // PARTS[name]), cols // PARTS[name])
+                grad, out = refs["g_" + name].at[:, here], refs["o_" + name].at[:, here]
+                red[f"{name}.{p}"] = Reduction(rows, groups, sems, grad, bufs, out)
         hbm_out = dict(a=ga_h, b=gb_h, c=gc_h, d0=gd0_h, d1=gd1_h)
-        at = dict.fromkeys(grads, 0)
+        at = dict.fromkeys(red, 0)
 
         def advance(name, number):
             if number > red[name].last:
@@ -327,7 +336,13 @@
             at[name] += 1
             red[name].step(number)
             if number == red[name].last:
-                store(refs["o_" + name], hbm_out[name])
+                parent, p = name.split(".")
+                cols = grads[parent][1] // PARTS[parent]
+                store(red[name].out, hbm_out[parent].at[:, pl.ds(int(p) * cols, cols)])
+
+        def begin(parent):
+            for p in range(PARTS[parent]):
+                advance(f"{parent}.{p}", 0)
 
         segf = seg[...].astype(F32)
         s.segf[...] = segf
@@ -338,8 +353,7 @@
 
         def project(rows):
             xb = s.x[rows, :]
-            s.xt[:, rows] = xb.T
-            qv = nn(xb, s.wqkv[0]) + bqv[0:1, :]
+            qv = (nn(xb, s.wqkv[0]) + bqv[0:1, :]) * score_c
             kv = nn(xb, s.wqkv[1])
             vv = nn(xb, s.wqkv[2]) + bqv[1:2, :]
             ql, kl, vl = qv.astype(BF16), kv.astype(BF16), vv.astype(BF16)
@@ -348,7 +362,6 @@
                 s.q[h, rows, :] = ql[:, cols]
                 s.k[h, rows, :] = kl[:, cols]
                 s.v[h, rows, :] = vl[:, cols]
-                s.kt[h, :, rows] = kl[:, cols].T
                 s.vt[h, :, rows] = vl[:, cols].T
 
         x_in[0].wait()
@@ -366,12 +379,9 @@
         weights = [across(wout_h, s.wout_o), across(win_h, s.win_o), across(wdown_h, s.wdown_o), across(bin_, s.bin_o)]
         launch(*weights)
 
-        def attend(i, _):
-            h = lax.rem(i, heads)
-            qi = lax.rem(other * (blocks // 2) + lax.div(i, heads), blocks)
+        def attend_head(h, qi):
             rows = blk(qi * qb, qb)
-            products = nt(s.k[h], s.q[h, rows, :]) * score_c
-            scores = jnp.where(s.kb[...] == s.segf[:, rows], products, MASKED_SCORE)
+            scores = jnp.where(s.kb[...] == s.segf[:, rows], nt(s.k[h], s.q[h, rows, :]), MASKED_SCORE)
             top = jnp.max(scores, 0, keepdims=True)
             weights_t = jnp.exp2(scores - top)
             inverse = 1.0 / jnp.sum(weights_t, 0, keepdims=True)
@@ -380,13 +390,17 @@
             mixed = nn(s.vt[h], low) * inverse
             s.mix[h, rows, :] = mixed.T.astype(BF16)
             s.inv[h, rows, :] = jnp.broadcast_to(inverse, (HD, qb)).T
+
+        def attend(i, _):
+            for h in range(heads):
+                attend_head(h, lax.rem(other * (blocks // 2) + i, blocks))
             return 0
 
         n_att = heads * blocks
-        lax.fori_loop(0, n_att // 2, attend, 0)
+        lax.fori_loop(0, blocks // 2, attend, 0)
         mix_out = [across(s.mix.at[h, pl.ds(ot0, half)], s.mo.at[h]) for h in range(heads)]
         launch(*mix_out)
-        lax.fori_loop(n_att // 2, n_att, attend, 0)
+        lax.fori_loop(blocks // 2, blocks, attend, 0)
         for c in weights_in:
             c.wait()
         for c in weights + mix_out:
@@ -476,7 +490,7 @@
             part[name].wait_recv()
             mine, theirs = refs["g_" + name], refs["gr_" + name]
             mine[...] = (mine[...].astype(F32) + theirs[...].astype(F32)).astype(BF16)
-            advance(name, 0)
+            begin(name)
 
         grad_block(s.gs_a, s.act.at[1], s.ddown)
         launch(part["a"])
@@ -493,13 +507,21 @@
         s.g_c[...] = tn(mine, s.dattn[...]).astype(BF16)
         join("c")
 
+        def turn(i, _):
+            rows = blk(i * qb, qb)
+            s.xt[:, rows] = s.x[rows, :].T
+            for h in range(heads):
+                s.kt[h, :, rows] = s.k[h, rows, :].T
+            return 0
+
+        lax.fori_loop(0, blocks, turn, 0)
         s.dkacc[...] = jnp.zeros_like(s.dkacc)
         s.dvacc[...] = jnp.zeros_like(s.dvacc)
         for h in range(heads):
             across(s.dmo.at[h], s.dmix.at[h, pl.ds(ot0, half)], dmix_slots[h]).wait_recv()
 
         def finish_head(h):
-            dk = (s.dkacc[h] * (HD ** (-0.5))).astype(BF16)
+            dk = (s.dkacc[h] * (1.0 / LOG2E)).astype(BF16)
             dv = s.dvacc[h].astype(BF16)
             s.dcat[h, :, HD : 2 * HD] = dk
             s.dcat[h, :, 2 * HD :] = dv
@@ -513,11 +535,15 @@
                 return 0
 
             lax.fori_loop(0, width // 128, body, 0)
+            begin("d0" if h == 0 else "d1")
 
         def advance_all(tokens):
             for token in tokens:
-                name, number = token.split(":") if ":" in token else (token[0], token[1:])
-                advance(name, int(number))
+                if token == "head0":
+                    finish_head(0)
+                else:
+                    name, number = token.split(":")
+                    advance(name, int(number))
 
         def attend_back(i, _):
             h = lax.div(i, blocks)
@@ -536,8 +562,6 @@
 
                 @pl.when(i == number)
                 def _():
-                    if number == blocks - 1:
-                        finish_head(0)
                     advance_all(tokens)
 
             return 0
@@ -617,7 +641,7 @@
                 small_step(int(token[2:]))
             else:
                 advance_all([token])
-        for name in grads:
+        for name in red:
             while at[name] <= red[name].last:
                 advance(name, at[name])
         for c in all_copies:

time: 80.3 us -> 78.5 us (0.978)
  Pallas kernels: 79.4 us -> 77.6 us
    pallas_call x1, Pallas kernels: 74.4 us -> 72.6 us  [on_device(): pl.pallas_call(kernel, out_shape=shapes, in_specs=[any_, any_, vmem, any_...]
where the time goes in v3:
time: 78.5 us; the launch traced here: 78.3 us
  Pallas kernels  77.6 us (99%)
    pallas_call x1, Pallas kernels, on_device(): pl.pallas_call(kernel, out_shape=shapes, in_specs=[any_, any_, vmem, any_...  72.6 us
    pallas_call x1, Pallas kernels, on_device(): finish_kernel(grads, half, width, hw)(*partial_results)  4.96 us

profile of v3, /device:TPU:0, one launch (start us, length us, event | category | flops | bytes accessed | tf_op | source)
XLA Modules:
  0.0 78.3 jit_solution(10991282240876409878)
XLA Ops:
  0.7 72.6 %shard_map.254 = (bf16[512,512]{1,0:T(8,128)(2,1)}, bf16[512,512]{1,0:T(8,128)(2,1)}, bf16[512,512]{1,0:T(8,128)(2,1)}, bf16[512,512]{1,0:T(8,128)(2,1)}, bf16[2...) custom-call(bf16[1024,512]{1,0:T(8,128)(2,1)} %x_h.1, ...), custom_call_target="tpu_custom_call" | custom-call | tf_op jit(solution)/shard_map/pallas_call | solution.py:756
  73.3 5.0 %shard_map.255 = (bf16[512,512]{1,0:T(8,128)(2,1)}, bf16[512,512]{1,0:T(8,128)(2,1)}, f32[3,512,256]{2,1,0:T(8,128)}, f32[256,512]{1,0:T(8,128)}, f32[512,512]{1...) custom-call(bf16[512,512]{1,0:T(8,128)(2,1)} %get-tuple-element.36.o, ...), custom_call_target="tpu_custom_call" | custom-call | tf_op jit(solution)/shard_map/pallas_call | solution.py:769
